TPU v7x, 512 devices: a 4x2x32 block of a 4x8x32 slice. The times are simulated.
512 devices in a mesh: member: 2 (over y), slab: 32 (over z), chan: 4 (over x), mode: 2 (over core).
Axes of the slice: x: 4, y: 2, z: 32, core: 2. Of those that a mesh axis runs over, the one named last changes fastest.
The devices are a block of a 4x8x32 slice.
Arguments:
- source_field: float32 [128, 1024, 1024], P(('member', 'chan'), 'slab', 'mode'), parts along dimension 0, may hold values from -6 to 6
- cotangent: float32 [128, 1024, 1024], P(('member', 'chan'), 'slab', 'mode'), parts along dimension 0, may hold values from -6 to 6
- spectral_weight: float32 [128, 64, 32, 2, 64], P(('member', 'chan'), None, 'mode', None, 'slab'), parts along dimension 0, may hold values from -12 to 12
- skip_gain: float32 [128], P(('member', 'chan')), parts along dimension 0, may hold values from 0.5 to 2
- channel_bias: float32 [128], P(('member', 'chan')), parts along dimension 0, may hold values from -0.5 to 0.5
- mode_limit: int32 [128, 2], P('member'), parts along dimension 0, may hold values from 16 to 32
- width_limit: int32 [128], P('member'), parts along dimension 0, may hold values from 32 to 64
Outputs:
- output: float32 [128, 1024, 1024], P(('member', 'chan'), 'slab', 'mode'), parts along dimension 0
- field_grad: float32 [128, 1024, 1024], P(('member', 'chan'), 'slab', 'mode'), parts along dimension 0
- spectral_grad: float32 [128, 64, 32, 2, 64], P(('member', 'chan'), None, 'mode', None, 'slab'), parts along dimension 0
- gate_grad: float32 [128], P(('member', 'chan')), parts along dimension 0
- bias_grad: float32 [128], P(('member', 'chan')), parts along dimension 0
There are 2 independent parts, one for each index of `member`. A program takes and returns all parts, laid end to end along the dimension named above; each array names one. Nothing has to cross between parts.
Inputs may be any that keep to these rules, and one draw needn't show every extreme that they name: `mode_limit`: never more than 32. `width_limit`: never more than 64.
All inputs are finite; a program needn't handle non-finite values.
Results may differ from a plain program's by a relative error of at most 0.00018.
Values sent between devices are 32-bit elements; how exact they have to be, the bound alone decides.
A program may use at most 64 MiB of HBM per device.

v0:
```python
import math

import jax
import jax.numpy as jnp
from jax import lax
from jax.sharding import PartitionSpec as P

precise = lax.Precision.HIGHEST


def in_blocks(x, dim, length):
    before, after = (x.shape[:dim], x.shape[dim + 1 :])
    return jnp.moveaxis(x.reshape(*before, length, -1, *after), dim, 0)


def sum_at_owner(x, axis, dim):
    tiles = in_blocks(x, dim, lax.axis_size(axis))
    arrived = lax.all_to_all(tiles, axis, split_axis=0, concat_axis=0, tiled=True)
    return arrived.sum(axis=0)


def from_everyone(x, axis):
    copies = jnp.broadcast_to(x, (lax.axis_size(axis), *x.shape))
    return lax.all_to_all(copies, axis, split_axis=0, concat_axis=0, tiled=True)


def in_order(tiles, dim):
    lengths = list(tiles.shape[1:])
    lengths[dim] *= tiles.shape[0]
    return jnp.moveaxis(tiles, 0, dim).reshape(lengths)


def gathered_copies(x, axis, dim):
    tiles = from_everyone(x, axis)
    return in_order(tiles, dim)


def taken_together(x, axis):
    everything = from_everyone(x, axis)
    return jnp.sum(everything, axis=0)


def packed_total(arrays, axis):
    ends = [0]
    for a in arrays:
        ends.append(ends[-1] + a.size)
    total = taken_together(jnp.concatenate([a.ravel() for a in arrays]), axis)
    return tuple((total[b:e].reshape(a.shape) for a, b, e in zip(arrays, ends, ends[1:])))


def column_table(extent, freq_count, first_cell, cell_count):
    cell_index = first_cell + jnp.arange(cell_count, dtype=jnp.int32)
    wave_index = jnp.arange(freq_count, dtype=jnp.int32)
    products = (cell_index[:, None] * wave_index[None, :] % extent).astype(jnp.float32)
    angles = products * (2.0 * math.pi / extent)
    return jnp.stack([jnp.cos(angles), -jnp.sin(angles)], axis=-1).reshape(
        cell_count, 2 * freq_count
    )


def row_tables(extent, freq_count, first_cell, cell_count):
    cell_index = first_cell + jnp.arange(cell_count, dtype=jnp.int32)
    column = jnp.arange(2 * freq_count, dtype=jnp.int32)
    wave_index = column + jnp.where(column >= freq_count, extent - 2 * freq_count, 0)
    products = (cell_index[:, None] * wave_index[None, :] % extent).astype(jnp.float32)
    angles = products * (2.0 * math.pi / extent)
    return (jnp.cos(angles), jnp.sin(angles))


def row_forward(lined, row_cos, row_sin):
    line_real = lined[:, 0]
    line_imag = lined[:, 1]
    out_real = jnp.dot(line_real, row_cos, precision=precise) + jnp.dot(
        line_imag, row_sin, precision=precise
    )
    out_imag = jnp.dot(line_imag, row_cos, precision=precise) - jnp.dot(
        line_real, row_sin, precision=precise
    )
    return jnp.stack([out_real, out_imag], axis=1)


def row_inverse(modes_in, row_cos, row_sin):
    mode_real = modes_in[:, 0]
    mode_imag = modes_in[:, 1]
    back_real = jnp.dot(mode_real, row_cos.T, precision=precise) - jnp.dot(
        mode_imag, row_sin.T, precision=precise
    )
    back_imag = jnp.dot(mode_real, row_sin.T, precision=precise) + jnp.dot(
        mode_imag, row_cos.T, precision=precise
    )
    return jnp.stack([back_real, back_imag], axis=1)


def contract(spectra, weight):
    spec_real = spectra[:, :, 0]
    spec_imag = spectra[:, :, 1]
    weight_real = weight[:, :, :, 0]
    weight_imag = weight[:, :, :, 1]
    out_real = jnp.einsum("iyx,ioyx->oyx", spec_real, weight_real, precision=precise) - jnp.einsum(
        "iyx,ioyx->oyx", spec_imag, weight_imag, precision=precise
    )
    out_imag = jnp.einsum("iyx,ioyx->oyx", spec_real, weight_imag, precision=precise) + jnp.einsum(
        "iyx,ioyx->oyx", spec_imag, weight_real, precision=precise
    )
    return jnp.stack([out_real, out_imag], axis=2)


def contract_back(grads, weight):
    grad_real = grads[:, :, 0]
    grad_imag = grads[:, :, 1]
    weight_real = weight[:, :, :, 0]
    weight_imag = weight[:, :, :, 1]
    back_real = jnp.einsum("oyx,ioyx->iyx", grad_real, weight_real, precision=precise) + jnp.einsum(
        "oyx,ioyx->iyx", grad_imag, weight_imag, precision=precise
    )
    back_imag = jnp.einsum("oyx,ioyx->iyx", grad_imag, weight_real, precision=precise) - jnp.einsum(
        "oyx,ioyx->iyx", grad_real, weight_imag, precision=precise
    )
    return jnp.stack([back_real, back_imag], axis=2)


def outer_grad(spectra, grads):
    spec_real = spectra[:, :, 0]
    spec_imag = spectra[:, :, 1]
    grad_real = grads[:, :, 0]
    grad_imag = grads[:, :, 1]
    real_side = jnp.einsum("iyx,oyx->ioyx", spec_real, grad_real) + jnp.einsum(
        "iyx,oyx->ioyx", spec_imag, grad_imag
    )
    imag_side = jnp.einsum("iyx,oyx->ioyx", spec_real, grad_imag) - jnp.einsum(
        "iyx,oyx->ioyx", spec_imag, grad_real
    )
    return jnp.stack([real_side, imag_side], axis=3)


def mode_weights(limit_rows, col_freq, row_freq, kx_count, cells_total):
    keep_cols = col_freq[None, :] < limit_rows[:, 0:1]
    keep_rows = (row_freq[None, :] < limit_rows[:, 1:2]) | (
        (kx_count - row_freq)[None, :] < limit_rows[:, 1:2]
    )
    scales = jnp.where(col_freq == 0, 1.0, 2.0).astype(jnp.float32) / cells_total
    joined = keep_cols[:, :, None] & keep_rows[:, None, :]
    return (joined.astype(jnp.float32) * scales[None, :, None])[:, :, None, :]


def read_mask(in_index, width_limit):
    return (in_index[:, None] < width_limit[None, :]).astype(jnp.float32)[:, :, None, None, None]


def local(
    source_field, cotangent, spectral_weight, skip_gain, channel_bias, mode_limit, width_limit
):
    channels, row_count, col_count = source_field.shape
    slab_count = lax.axis_size("slab")
    mode_count = lax.axis_size("mode")
    slab_index = lax.axis_index("slab")
    mode_index = lax.axis_index("mode")
    chan_index = lax.axis_index("chan")
    local_freq = spectral_weight.shape[2]
    local_kx = spectral_weight.shape[4]
    freq_count = local_freq * mode_count
    kx_count = local_kx * slab_count
    all_rows = row_count * slab_count
    all_cols = col_count * mode_count
    column_tab = column_table(all_cols, freq_count, mode_index * col_count, col_count)
    row_cos, row_sin = row_tables(all_rows, freq_count, slab_index * row_count, row_count)

    def spectrum(values):
        partial_cols = jnp.einsum("chw,wk->ckh", values, column_tab, precision=precise)
        summed_cols = sum_at_owner(partial_cols, "mode", 1)
        paired = summed_cols.reshape(values.shape[0] * local_freq, 2, row_count)
        spectra = sum_at_owner(row_forward(paired, row_cos, row_sin), "slab", 2)
        return spectra.reshape(values.shape[0], local_freq, 2, local_kx)

    def synthesis(modes_in):
        whole_modes = gathered_copies(modes_in, "slab", 3)
        rebuilt = row_inverse(
            whole_modes.reshape(channels * local_freq, 2, kx_count), row_cos, row_sin
        )
        rebuilt = rebuilt.reshape(channels, 2 * local_freq, row_count)
        gathered = lax.all_gather(rebuilt, "mode", axis=1, tiled=True)
        return jnp.einsum("ckh,wk->chw", gathered, column_tab, precision=precise)

    in_index = chan_index * channels + jnp.arange(channels, dtype=jnp.int32)
    col_freq = mode_index * local_freq + jnp.arange(local_freq, dtype=jnp.int32)
    row_freq = slab_index * local_kx + jnp.arange(local_kx, dtype=jnp.int32)
    limit_rows = lax.dynamic_slice_in_dim(mode_limit, chan_index * channels, channels, 0)
    weights = mode_weights(limit_rows, col_freq, row_freq, kx_count, all_rows * all_cols)
    reads = read_mask(in_index, width_limit)
    masked_weight = spectral_weight * reads
    spectra = spectrum(source_field)
    out_modes = sum_at_owner(contract(spectra, masked_weight), "chan", 0) * weights
    branch = synthesis(out_modes)
    skip_scale = skip_gain[:, None, None]
    summed = branch + skip_scale * source_field + channel_bias[:, None, None]
    output, gelu_back = jax.vjp(jax.nn.gelu, summed)
    grad_sum = gelu_back(cotangent)[0]
    grad_modes = spectrum(grad_sum) * weights
    all_grads = lax.all_gather(grad_modes, "chan", axis=0, tiled=True)
    spectral_grad = outer_grad(spectra, all_grads) * reads
    field_grad = synthesis(contract_back(all_grads, masked_weight)) + skip_scale * grad_sum
    gate_grad, bias_grad = packed_total(
        (jnp.sum(grad_sum * source_field, axis=(1, 2)), jnp.sum(grad_sum, axis=(1, 2))),
        ("slab", "mode"),
    )
    return (output, field_grad, spectral_grad, gate_grad, bias_grad)


def solution(mesh):
    in_specs = (
        P(("member", "chan"), "slab", "mode"),
        P(("member", "chan"), "slab", "mode"),
        P(("member", "chan"), None, "mode", None, "slab"),
        P(("member", "chan")),
        P(("member", "chan")),
        P("member", None),
        P("member"),
    )
    out_specs = (
        P(("member", "chan"), "slab", "mode"),
        P(("member", "chan"), "slab", "mode"),
        P(("member", "chan"), None, "mode", None, "slab"),
        P(("member", "chan")),
        P(("member", "chan")),
    )
    return jax.shard_map(local, mesh=mesh, in_specs=in_specs, out_specs=out_specs, check_vma=False)
```

profile of v0, /device:TPU:33, one launch (start us, length us, event | category | flops | bytes accessed | tf_op | source)
XLA Modules:
  0.0 276.8 jit_solution(1268335611146593142)
XLA Ops:
  1.2 2.2 convolution_bitcast_fusion.1
  3.8 0.9 reshape.329
  4.7 44.8 %all-to-all-start = ((f32[2,1,16384]{2,1,0:T(1,128)}), f32[2,1,16384]{2,1,0:T(1,128)S(1)}, u32[]{:S(2)}, u32[]{:S(2)}) async-start(f32[2,1,16384]{2,1,0:T(1,128)} %reshape.329), calls=%async_computation | async-start | bytes 262144 | tf_op jit(solution)/shard_map/all_to_all | solution.py:18
  49.5 1.1 all-to-all-done
  50.6 0.6 broadcast.358
  51.2 1.1 reduce.9
  52.9 0.4 fusion.51
  53.4 0.4 fusion.53
  53.8 0.4 convolution_subtract_fusion.1
  54.3 0.4 convolution_add_fusion.3
  54.8 0.7 maximum_bitcast_fusion
  55.5 5.5 %all-to-all-start.1 = ((f32[32,256,2,2]{1,3,2,0:T(2,128)}), f32[32,256,2,2]{1,3,2,0:T(2,128)S(1)}, u32[]{:S(2)}, u32[]{:S(2)}) async-start(f32[32,256,2,2]{1,3,2,0:T(2,128)} %maximum_bitcast_fusion), calls=%async_computation.1 | async-start | bytes 262144 | tf_op jit(solution)/shard_map/all_to_all | solution.py:18
  61.3 0.6 copy-done.4
  62.3 27.9 %all-to-all-done.1 = f32[32,256,2,2]{1,3,2,0:T(2,128)S(1)} async-done(((f32[32,256,2,2]{1,3,2,0:T(2,128)}), f32[32,256,2,2]{1,3,2,0:T(2,128)S(1)}, u32[]{:S(2)}, u32[]{:S(2)}) %all-to-all-start.1) | async-done | bytes 131104 | tf_op jit(solution)/shard_map/all_to_all | solution.py:18
  90.5 0.5 fusion.17
  91.0 0.5 fusion.19
  91.5 0.5 fusion.21
  92.1 0.5 fusion.23
  93.0 0.8 reshape.331
  93.8 4.3 %all-to-all-start.2 = ((f32[4,1,1024]{2,1,0:T(1,128)}), f32[4,1,1024]{2,1,0:T(1,128)S(1)}, u32[]{:S(2)}, u32[]{:S(2)}) async-start(f32[4,1,1024]{2,1,0:T(1,128)} %reshape.331), calls=%async_computation.2 | async-start | bytes 32768 | tf_op jit(solution)/shard_map/all_to_all | solution.py:18
  98.1 4.1 %all-to-all-done.2 = f32[4,1,1024]{2,1,0:T(1,128)S(1)} async-done(((f32[4,1,1024]{2,1,0:T(1,128)}), f32[4,1,1024]{2,1,0:T(1,128)S(1)}, u32[]{:S(2)}, u32[]{:S(2)}) %all-to-all-start.2) | async-done | bytes 16416 | tf_op jit(solution)/shard_map/all_to_all | solution.py:18
  102.3 0.7 reduce.10
  103.9 30.2 %all_to_all.41 = f32[32,1,1024]{2,1,0:T(1,128)S(1)} all-to-all(f32[32,1,1024]{2,1,0:T(1,128)S(1)} %reshape.333), channel_id=1, replica_groups=mesh['member'=2,'slab'=32,'chan'=4,'mode'=2] {'slab'}, dimensions={0} | all-to-all | bytes 262144 | tf_op jit(solution)/shard_map/all_to_all | solution.py:24
  134.1 1.0 reduce.11
  137.6 7.6 %all_gather.9 = f32[16,64,32]{2,0,1:T(8,128)S(1)} all-gather(f32[16,32,32]{2,0,1:T(8,128)S(1)} %copy.218), channel_id=1, replica_groups=mesh['member'=2,'slab'=32,'chan'=4,'mode'=2] {'mode'}, dimensions={1}, use_global_device_ids=true | all-gather | bytes 196608 | tf_op jit(solution)/shard_map/all_gather | solution.py:181
  145.2 4.3 %multiply_reduce_fusion = (f32[16]{0:T(128)S(1)}, f32[16]{0:T(128)S(1)}, f32[16,32,512]{2,1,0:T(8,128)S(1)}, f32[16,32,512]{2,1,0:T(8,128)}) fusion(f32[16,32,512]{2,1,0:T(8,128)S(1)} %copy-done.1, f32[16,32,512]{2,1,0:T(8,128)} %param.8, f32[16]{0:T(128)S(1)} %copy-done.5, f32[16]{0:T(128)S(1)} %copy-done.3, f32[512,64,1]{0,1,2:T(8,128)S(1)} %reshape.313, ...), kind=kOutput, calls=%fused_computation.25 | convolution fusion | flops 208142304 | bytes 4456704 | tf_op jit(solution)/shard_map/ckh,wk->chw/dot_general | solution.py:182
  149.5 1.0 convolution_bitcast_fusion
  151.2 3.9 %all_to_all.42 = f32[2,1,16384]{2,1,0:T(1,128)S(1)} all-to-all(f32[2,1,16384]{2,1,0:T(1,128)S(1)} %reshape.335), channel_id=1, replica_groups=mesh['member'=2,'slab'=32,'chan'=4,'mode'=2] {'mode'}, dimensions={0} | all-to-all | bytes 262144 | tf_op jit(solution)/shard_map/all_to_all | solution.py:18
  155.0 1.1 reduce.12
  157.2 0.4 fusion.47
  157.6 0.4 convolution_subtract_fusion
  158.1 0.4 convolution_add_fusion.2
  158.6 0.7 maximum_bitcast_fusion.1
  159.3 4.8 %all-to-all-start.5 = ((f32[32,256,2,2]{1,3,2,0:T(2,128)}), f32[32,256,2,2]{1,3,2,0:T(2,128)S(1)}, u32[]{:S(2)}, u32[]{:S(2)}) async-start(f32[32,256,2,2]{1,3,2,0:T(2,128)} %maximum_bitcast_fusion.1), calls=%async_computation.5 | async-start | bytes 262144 | tf_op jit(solution)/shard_map/all_to_all | solution.py:18
  164.5 28.8 %all-to-all-done.5 = f32[32,256,2,2]{1,3,2,0:T(2,128)S(1)} async-done(((f32[32,256,2,2]{1,3,2,0:T(2,128)}), f32[32,256,2,2]{1,3,2,0:T(2,128)S(1)}, u32[]{:S(2)}, u32[]{:S(2)}) %all-to-all-start.5) | async-done | bytes 131104 | tf_op jit(solution)/shard_map/all_to_all | solution.py:18
  193.4 0.6 broadcast_in_dim.47
  194.0 7.3 %all-to-all-start.7 = ((f32[64,1,32]{2,1,0:T(1,128)}), f32[64,1,32]{2,1,0:T(1,128)S(1)}, u32[]{:S(2)}, u32[]{:S(2)}) async-start(f32[64,1,32]{2,1,0:T(1,128)} %broadcast_in_dim.47), calls=%async_computation.7 | async-start | bytes 65536 | tf_op jit(solution)/shard_map/all_to_all | solution.py:24
  201.5 10.3 %all_gather.10 = f32[64,16,2,2]{1,3,2,0:T(2,128)S(1)} all-gather(f32[16,16,2,2]{1,3,2,0:T(2,128)S(1)} %copy.225), channel_id=1, replica_groups=mesh['member'=2,'slab'=32,'chan'=4,'mode'=2] {'chan'}, dimensions={0}, use_global_device_ids=true | all-gather | bytes 20480 | tf_op jit(solution)/shard_map/all_gather | solution.py:199
  211.9 1.9 add_bitcast_fusion
  214.7 1.1 reshape.337
  215.7 8.1 %all-to-all-done.7 = f32[64,1,32]{2,1,0:T(1,128)S(1)} async-done(((f32[64,1,32]{2,1,0:T(1,128)}), f32[64,1,32]{2,1,0:T(1,128)S(1)}, u32[]{:S(2)}, u32[]{:S(2)}) %all-to-all-start.7) | async-done | bytes 8224 | tf_op jit(solution)/shard_map/all_to_all | solution.py:24
  223.8 13.7 %all-to-all-start.6 = ((f32[32,1,1024]{2,1,0:T(1,128)}), f32[32,1,1024]{2,1,0:T(1,128)S(1)}, u32[]{:S(2)}, u32[]{:S(2)}) async-start(f32[32,1,1024]{2,1,0:T(1,128)} %reshape.337), calls=%async_computation.6 | async-start | bytes 262144 | tf_op jit(solution)/shard_map/all_to_all | solution.py:24
  237.6 0.6 fusion.132
  238.2 1.1 maximum_multiply_fusion
  239.3 24.1 %all-to-all-done.6 = f32[32,1,1024]{2,1,0:T(1,128)S(1)} async-done(((f32[32,1,1024]{2,1,0:T(1,128)}), f32[32,1,1024]{2,1,0:T(1,128)S(1)}, u32[]{:S(2)}, u32[]{:S(2)}) %all-to-all-start.6) | async-done | bytes 131104 | tf_op jit(solution)/shard_map/all_to_all | solution.py:24
  263.4 1.0 reduce.13
  266.9 7.8 %all_gather.11 = f32[16,64,32]{2,0,1:T(8,128)S(1)} all-gather(f32[16,32,32]{2,0,1:T(8,128)S(1)} %copy.228), channel_id=1, replica_groups=mesh['member'=2,'slab'=32,'chan'=4,'mode'=2] {'mode'}, dimensions={1}, use_global_device_ids=true | all-gather | bytes 196608 | tf_op jit(solution)/shard_map/all_gather | solution.py:181
  274.7 2.1 convolution_add_fusion
  (106 shorter events, 12.2 us)
Async XLA Ops:
  0.6 60.4 %copy-start = (s32[64,2]{0,1:T(2,128)S(1)}, s32[64,2]{0,1:T(2,128)}, u32[]{:S(2)}) copy-start(s32[64,2]{0,1:T(2,128)} %param.12) | copy-start | bytes 1540
  4.7 45.9 %all-to-all-start = ((f32[2,1,16384]{2,1,0:T(1,128)}), f32[2,1,16384]{2,1,0:T(1,128)S(1)}, u32[]{:S(2)}, u32[]{:S(2)}) async-start(f32[2,1,16384]{2,1,0:T(1,128)} %reshape.329), calls=%async_computation | async-start | bytes 262144 | tf_op jit(solution)/shard_map/all_to_all | solution.py:18
  54.3 7.7 %copy-start.2 = (f32[16,64,16,2,2]{1,4,3,2,0:T(2,128)S(1)}, f32[16,64,16,2,2]{1,4,3,2,0:T(2,128)}, u32[]{:S(2)}) copy-start(f32[16,64,16,2,2]{1,4,3,2,0:T(2,128)} %param.9) | copy-start | bytes 786436
  55.5 34.7 %all-to-all-start.1 = ((f32[32,256,2,2]{1,3,2,0:T(2,128)}), f32[32,256,2,2]{1,3,2,0:T(2,128)S(1)}, u32[]{:S(2)}, u32[]{:S(2)}) async-start(f32[32,256,2,2]{1,3,2,0:T(2,128)} %maximum_bitcast_fusion), calls=%async_computation.1 | async-start | bytes 262144 | tf_op jit(solution)/shard_map/all_to_all | solution.py:18
  61.2 0.7 copy-start.4
  93.8 8.5 %all-to-all-start.2 = ((f32[4,1,1024]{2,1,0:T(1,128)}), f32[4,1,1024]{2,1,0:T(1,128)S(1)}, u32[]{:S(2)}, u32[]{:S(2)}) async-start(f32[4,1,1024]{2,1,0:T(1,128)} %reshape.331), calls=%async_computation.2 | async-start | bytes 32768 | tf_op jit(solution)/shard_map/all_to_all | solution.py:18
  136.3 8.9 %copy-start.1 = (f32[16,32,512]{2,1,0:T(8,128)S(1)}, f32[16,32,512]{2,1,0:T(8,128)}, u32[]{:S(2)}) copy-start(f32[16,32,512]{2,1,0:T(8,128)} %param.7) | copy-start | bytes 3145732
  137.6 7.7 %copy-start.3 = (f32[16]{0:T(128)S(1)}, f32[16]{0:T(128)}, u32[]{:S(2)}) copy-start(f32[16]{0:T(128)} %param.10) | copy-start | bytes 196
  137.6 7.7 %copy-start.5 = (f32[16]{0:T(128)S(1)}, f32[16]{0:T(128)}, u32[]{:S(2)}) copy-start(f32[16]{0:T(128)} %param.11) | copy-start | bytes 196
  159.3 34.0 %all-to-all-start.5 = ((f32[32,256,2,2]{1,3,2,0:T(2,128)}), f32[32,256,2,2]{1,3,2,0:T(2,128)S(1)}, u32[]{:S(2)}, u32[]{:S(2)}) async-start(f32[32,256,2,2]{1,3,2,0:T(2,128)} %maximum_bitcast_fusion.1), calls=%async_computation.5 | async-start | bytes 262144 | tf_op jit(solution)/shard_map/all_to_all | solution.py:18
  194.0 29.8 %all-to-all-start.7 = ((f32[64,1,32]{2,1,0:T(1,128)}), f32[64,1,32]{2,1,0:T(1,128)S(1)}, u32[]{:S(2)}, u32[]{:S(2)}) async-start(f32[64,1,32]{2,1,0:T(1,128)} %broadcast_in_dim.47), calls=%async_computation.7 | async-start | bytes 65536 | tf_op jit(solution)/shard_map/all_to_all | solution.py:24
  223.8 39.6 %all-to-all-start.6 = ((f32[32,1,1024]{2,1,0:T(1,128)}), f32[32,1,1024]{2,1,0:T(1,128)S(1)}, u32[]{:S(2)}, u32[]{:S(2)}) async-start(f32[32,1,1024]{2,1,0:T(1,128)} %reshape.337), calls=%async_computation.6 | async-start | bytes 262144 | tf_op jit(solution)/shard_map/all_to_all | solution.py:24
where the time goes:
time: 278 us; the launch traced here: 277 us
  waiting for transfers between devices  94.1 us (34%)
  starting transfers between devices  80.4 us (29%)
  blocking collectives  59.7 us (21%)
  matrix products  17.5 us (6%)
  local copies, waits for them, and re-layouts  13.2 us (5%)
  other arithmetic  10.6 us (4%)
    all_to_all x4, waiting for transfers between devices, sum_at_owner(): lax.all_to_all(tiles, axis, split_axis=0, concat_axis=0, tiled=True)  61.9 us
    all_to_all x4, starting transfers between devices, sum_at_owner(): lax.all_to_all(tiles, axis, split_axis=0, concat_axis=0, tiled=True)  59.4 us
    all_to_all x2, waiting for transfers between devices, from_everyone(): return lax.all_to_all(copies, axis, split_axis=0, concat_axis=0, tiled=True)  32.2 us
    all_to_all x1, blocking collectives, from_everyone(): return lax.all_to_all(copies, axis, split_axis=0, concat_axis=0, tiled=True)  30.2 us
    all_to_all x2, starting transfers between devices, from_everyone(): return lax.all_to_all(copies, axis, split_axis=0, concat_axis=0, tiled=True)  21 us
    all_gather x2, blocking collectives, synthesis(): gathered = lax.all_gather(rebuilt, 'mode', axis=1, tiled=True)  15.4 us
    all_gather x1, blocking collectives, local(): all_grads = lax.all_gather(grad_modes, 'chan', axis=0, tiled=True)  10.3 us
    dot_general x2, matrix products, synthesis(): return jnp.einsum('ckh,wk->chw', gathered, column_tab, precision=precise)  6.39 us
  transfers between devices with their start and end apart: 6, of which 6 were waited for; matrix products, arithmetic and copies ran while one was open for 3% of the time, Pallas kernels for 0%

commit v1 on v0

v1 whole, which is shorter than its diff:
```python
import functools
import math

import jax
import jax.numpy as jnp
from jax import lax
from jax.experimental import pallas as pl
from jax.experimental.pallas import tpu as pltpu
from jax.sharding import PartitionSpec as P

MESH = pl.DeviceIdType.MESH
LANES = 128
GELU_SLOPE = math.sqrt(2.0 / math.pi)
GELU_CUBE = 0.044715


def split(x):
    high = x.astype(jnp.bfloat16)
    low = (x - high.astype(jnp.float32)).astype(jnp.bfloat16)
    return high, low


def dot3(a, b):
    (ah, al), (bh, bl) = a, b
    dot = functools.partial(jnp.dot, preferred_element_type=jnp.float32)
    return dot(ah, bh) + (dot(ah, bl) + dot(al, bh))


def sine(turns, extent):
    half, quarter = extent // 2, extent // 4
    t = ((turns + half) & (extent - 1)) - half
    t = jnp.where(t > quarter, half - t, jnp.where(t < -quarter, -half - t, t))
    v = t.astype(jnp.float32) * (2.0 * math.pi / extent)
    s = v * v
    poly = -2.5052108e-8
    for c in (2.7557319e-6, -1.9841270e-4, 8.3333333e-3, -1.6666667e-1, 1.0):
        poly = poly * s + c
    return poly * v


def iota(shape, dim):
    return lax.broadcasted_iota(jnp.int32, shape, dim)


def kernel(
    dims,
    x_hbm, cot_hbm, w_hbm, gain, bias, limit, width,
    out_hbm, fgrad_hbm, sgrad_hbm, gate_ref, bgrad_ref,
    xv, cv, wv, gv, ov, tch, tcl, tth, ttl, fh, fl, fth, ftl,
    wt, zs, sv, sgv,
    own_cols, tx_cols, rx_cols, tx_rows, rx_rows, tx_chan, rx_chan, tile_tx, rx_modes,
    own_g, rx_g, g_chan, red_pair, red_all,
    lsem, osem, msend, mrecv, ssend, srecv, csend, crecv,
):
    slabs, chans, modes, rows, cols = dims
    chunk = 4 * rows
    me, ch, mo = lax.axis_index("slab"), lax.axis_index("chan"), lax.axis_index("mode")
    other = 1 - mo
    all_rows, all_cols = slabs * rows, modes * cols
    kx_count = 2 * slabs

    loads = [
        pltpu.make_async_copy(x_hbm, xv, lsem.at[0]),
        pltpu.make_async_copy(cot_hbm, cv, lsem.at[1]),
        pltpu.make_async_copy(w_hbm, wv, lsem.at[2]),
    ]
    for load in loads:
        load.start()

    barrier = pltpu.get_barrier_semaphore()

    def greet(k, carry):
        pl.semaphore_signal(barrier, inc=1, device_id={"slab": lax.rem(me + k, slabs)}, device_id_type=MESH)
        return carry

    lax.fori_loop(1, slabs, greet, 0)
    for k in range(1, chans):
        pl.semaphore_signal(barrier, inc=1, device_id={"chan": lax.rem(ch + k, chans)}, device_id_type=MESH)
    pl.semaphore_signal(barrier, inc=1, device_id={"mode": other}, device_id_type=MESH)

    def to_mode(slot, src, dst):
        return pltpu.make_async_remote_copy(
            src_ref=src, dst_ref=dst, send_sem=msend.at[slot], recv_sem=mrecv.at[slot],
            device_id={"mode": other}, device_id_type=MESH,
        )

    def to_slabs(slot, src_of, dst):
        def one(n, carry):
            far = slabs // 2
            k = jnp.where(n % 2 == 0, far - n // 2, far + (n + 1) // 2)
            pltpu.make_async_remote_copy(
                src_ref=src_of(k), dst_ref=dst.at[slabs - k], send_sem=ssend.at[slot], recv_sem=srecv.at[slot],
                device_id={"slab": lax.rem(me + k, slabs)}, device_id_type=MESH,
            ).start()
            return carry

        lax.fori_loop(0, slabs - 1, one, 0)

    def wait_bytes(ref, sem):
        pltpu.make_async_copy(ref, ref, sem).wait()

    lane = iota((8, LANES), 1)
    real_part = lane % 32 < 16

    def turned(v):
        re = iota(v.shape, 1) % 32 < 16
        return jnp.where(re, pltpu.roll(v, LANES - 16, 1), -pltpu.roll(v, 16, 1))

    def column_angles(n, w):
        holder = jnp.where(n < LANES, mo, other)
        freq = holder * 16 + n % 16
        cell = mo * cols + w
        return freq * cell + jnp.where(n % 32 < 16, all_cols // 4, all_cols // 2)

    shape = (cols, 2 * LANES)
    tch[...], tcl[...] = split(sine(column_angles(iota(shape, 1), iota(shape, 0)), all_cols))

    def row_angles(k, n, mirror):
        kx = 2 * lax.rem(me + k // 8, slabs) + (k % 8) // 4
        kx = jnp.where(kx < kx_count // 2, kx, kx + all_rows - kx_count)
        half = LANES
        cell = me * rows + n % rows
        angle = kx * cell + jnp.where(n < half, all_rows // 4, 0)
        same = (k % 4) == ((n % half) // rows)
        return jnp.where(same, sine(angle, all_rows), 0.0)

    shape = (8 * slabs, 2 * LANES)
    fh[...], fl[...] = split(row_angles(iota(shape, 0), iota(shape, 1), False))

    def column_forward(a, values):
        d = dot3(split(values), (tch[...], tcl[...]))
        block = (iota((rows, 2 * LANES), 1) % LANES) // 32
        packed = d[:rows]
        for b in range(1, 4):
            packed = jnp.where(block == b, d[b * rows : (b + 1) * rows], packed)
        own_cols[pl.ds(a * rows, rows), :] = packed[:, :LANES]
        return packed[:, LANES:]

    loads[0].wait()

    def first_chunk(a, carry):
        values = xv[pl.ds(a * chunk, chunk), :]
        tx_cols[0, pl.ds(a * rows, rows), :] = column_forward(a, values)
        return carry

    lax.fori_loop(0, 4, first_chunk, 0)
    pl.semaphore_wait(barrier, slabs - 1 + chans - 1 + 1)

    def rows_forward(turn):
        copy = to_mode(turn, tx_cols.at[turn], rx_cols.at[turn])
        copy.start()
        copy.wait()
        lined = own_cols[...] + rx_cols[turn]
        both = jnp.concatenate([lined, turned(lined)], axis=0)
        partial = dot3((fh[...], fl[...]), split(both))
        tx_rows[turn] = partial.reshape(slabs, 8, LANES)
        to_slabs(turn, lambda k: tx_rows.at[turn, k], rx_rows.at[turn])

    def owned(turn):
        wait_bytes(rx_rows.at[turn, pl.ds(1, slabs - 1)], srecv.at[turn])
        total = tx_rows[turn, 0]
        for j in range(1, slabs):
            total = total + rx_rows[turn, j]
        return total

    rows_forward(0)

    shape = (2 * LANES, cols)
    tth[...], ttl[...] = split(sine(column_angles(iota(shape, 0), iota(shape, 1)), all_cols))
    shape = (2 * LANES, 8 * slabs)
    fth[...], ftl[...] = split(row_angles(iota(shape, 1), iota(shape, 0), True))

    sub = iota((8, LANES), 0)
    keep_col = jnp.zeros((8, LANES), jnp.int32)
    keep_row = jnp.zeros((8, LANES), jnp.int32)
    for c in range(16):
        here = (sub % 4 == c // 4) & (lane // 32 == c % 4)
        keep_col = jnp.where(here, limit[0, ch * 16 + c], keep_col)
        keep_row = jnp.where(here, limit[1, ch * 16 + c], keep_row)
    col_freq = mo * 16 + lane % 16
    row_freq = me * 2 + sub // 4
    kept = (col_freq < keep_col) & ((row_freq < keep_row) | (kx_count - row_freq < keep_row))
    scale = jnp.where(col_freq == 0, 1.0, 2.0) / (all_rows * all_cols)
    weights = jnp.where(kept, scale, 0.0)

    sub16 = iota((16, LANES), 0)
    lane16 = iota((16, LANES), 1)
    reads = jnp.zeros((16, LANES), jnp.int32)
    for o in range(16 * chans):
        reads = jnp.where((sub16 == o // 4) & (lane16 // 32 == o % 4), width[o], reads)

    loads[2].wait()

    def weights_in(pair, carry):
        parts = []
        for t in range(4):
            for p in range(2):
                parts.append(wv[2 * pair + t // 2, pl.ds(2 * p + t % 2, 16, stride=4), :])
        zs[...] = jnp.concatenate(parts, axis=0).T
        by_low = [zs[pl.ds(b, 16, stride=4), :] for b in range(4)]
        for t in range(4):
            i = 2 * pair + t // 2
            tile = jnp.zeros((16, LANES), jnp.float32)
            for b in range(4):
                shift = 32 * ((b - t) % 4)
                moved = pltpu.roll(by_low[b], shift, 1) if shift else by_low[b]
                tile = jnp.where(lane16 // 32 == b, moved, tile)
            tile = jnp.where(ch * 16 + i < reads, tile, 0.0)
            for d in range(chans):
                wt[i, d, pl.ds(4 * (t % 2), 4), :] = tile[4 * d : 4 * d + 4]
        return carry

    lax.fori_loop(0, 8, weights_in, 0)

    spectra = owned(0)
    for a in range(4):
        e = jnp.where(
            sub < 4,
            jnp.broadcast_to(spectra[a : a + 1], (8, LANES)),
            jnp.broadcast_to(spectra[4 + a : 5 + a], (8, LANES)),
        )
        rolled = [e] + [pltpu.roll(e, 16 * m, 1) for m in range(1, 8)]
        for q in range(8):
            copies = rolled[(0 - q) % 8]
            for t in range(1, 8):
                copies = jnp.where(lane // 16 == t, rolled[(t - q) % 8], copies)
            sv[4 * a + q // 2, q % 2] = copies

    zero = jnp.zeros((8, LANES), jnp.float32)

    def contract(i, sums):
        s_re, s_im = sv[i, 0], sv[i, 1]
        first = tuple(sums[d] + s_re * wt[i, d] for d in range(chans))
        second = tuple(sums[chans + d] + s_im * wt[i, d] for d in range(chans))
        return first + second

    sums = lax.fori_loop(0, 16, contract, (zero,) * (2 * chans), unroll=4)
    for d in range(chans):
        tx_chan[d] = sums[d] - turned(sums[chans + d])

    def to_chan(slot, k, src, dst):
        return pltpu.make_async_remote_copy(
            src_ref=src, dst_ref=dst, send_sem=csend.at[slot], recv_sem=crecv.at[slot],
            device_id={"chan": lax.rem(ch + k, chans)}, device_id_type=MESH,
        )

    for k in range(1, chans):
        to_chan(0, k, tx_chan.at[lax.rem(ch + k, chans)], rx_chan.at[chans - 1 - k]).start()
    wait_bytes(rx_chan, crecv.at[0])
    modes_out = tx_chan[ch]
    for k in range(chans - 1):
        modes_out = modes_out + rx_chan[k]

    def everywhere(turn, tile):
        tile_tx[turn] = tile
        rx_modes[turn, 0] = tile
        to_slabs(2 + turn, lambda k: tile_tx.at[turn], rx_modes.at[turn])

    def rows_back(turn):
        wait_bytes(rx_modes.at[turn, pl.ds(1, slabs - 1)], srecv.at[2 + turn])
        found = rx_modes[turn].reshape(8 * slabs, LANES)
        both = dot3((fth[...], ftl[...]), split(found))
        own_g[turn] = both[:LANES] - turned(both[LANES:])
        copy = to_mode(2 + turn, own_g.at[turn], rx_g.at[turn])
        copy.start()
        copy.wait()

    def column_back(turn, a):
        g = jnp.concatenate(
            [own_g[turn, pl.ds(a * rows, rows), :], rx_g[turn, pl.ds(a * rows, rows), :]], axis=1
        )
        block = (iota(g.shape, 1) % LANES) // 32
        spread = jnp.concatenate([jnp.where(block == b, g, 0.0) for b in range(4)], axis=0)
        return dot3(split(spread), (tth[...], ttl[...]))

    everywhere(0, modes_out * weights)
    loads[1].wait()
    rows_back(0)

    def gelu_chunk(a, carry):
        gates, biases = carry
        branch = column_back(0, a)
        grads = []
        for b in range(4):
            c = 4 * a + b
            here = pl.ds(c * rows, rows)
            x = xv[here, :]
            v = branch[b * rows : (b + 1) * rows] + gain[c] * x + bias[c]
            v2 = v * v
            t = jnp.tanh(GELU_SLOPE * (v + GELU_CUBE * (v2 * v)))
            cdf = 0.5 * (1.0 + t)
            ov[here, :] = v * cdf
            slope = cdf + (0.5 * GELU_SLOPE) * (v * (1.0 - t * t)) * (1.0 + (3.0 * GELU_CUBE) * v2)
            grad = cv[here, :] * slope
            gv[here, :] = grad
            grads.append(grad)
            gate = jnp.sum(jnp.sum(grad * x, axis=0, keepdims=True), axis=1, keepdims=True)
            plain = jnp.sum(jnp.sum(grad, axis=0, keepdims=True), axis=1, keepdims=True)
            spot = iota((1, LANES), 1) == c
            gates = jnp.where(spot, gate, gates)
            biases = jnp.where(spot, plain, biases)
        tx_cols[1, pl.ds(a * rows, rows), :] = column_forward(a, jnp.concatenate(grads, axis=0))
        here = pl.ds(a * chunk, chunk)
        pltpu.make_async_copy(ov.at[here, :], out_hbm.at[here, :], osem.at[0]).start()
        return gates, biases

    empty = jnp.zeros((1, LANES), jnp.float32)
    gates, biases = lax.fori_loop(0, 4, gelu_chunk, (empty, empty))
    rows_forward(1)

    red_pair[0] = jnp.concatenate([gates, biases], axis=0)
    copy = to_mode(4, red_pair.at[0], red_pair.at[1])
    copy.start()
    copy.wait()
    red_pair[2] = red_pair[0] + red_pair[1]
    to_slabs(4, lambda k: red_pair.at[2], red_all)

    g_chan[ch] = owned(1) * weights
    for k in range(1, chans):
        to_chan(1, k, g_chan.at[ch], g_chan.at[ch]).start()
    wait_bytes(g_chan.at[pl.ds(0, chans - 1)], crecv.at[1])
    g_all = [g_chan[d] for d in range(chans)]
    g_turned = [turned(g) for g in g_all]

    def contract_back(i):
        first, second = zero, zero
        for d in range(chans):
            w = wt[i, d]
            first = first + w * g_all[d]
            second = second + w * g_turned[d]
        v = jnp.where(real_part, first + pltpu.roll(first, 16, 1), second + pltpu.roll(second, 16, 1))
        v = v + pltpu.roll(v, 32, 1)
        return v + pltpu.roll(v, 64, 1)

    back = zero
    for a in range(4):
        m = contract_back(4 * a)
        for b in range(1, 4):
            m = jnp.where(lane // 32 == b, contract_back(4 * a + b), m)
        for x in range(2):
            row = jnp.sum(m[4 * x : 4 * x + 4], axis=0, keepdims=True)
            back = jnp.where(sub == 4 * x + a, jnp.broadcast_to(row, (8, LANES)), back)
    everywhere(1, back)

    def weights_out(pair, carry):
        tiles = []
        for t in range(4):
            i = 2 * pair + t // 2
            if t % 2 == 0:
                s_re, s_im = sv[i, 0], sv[i, 1]
                made = [s_re * g_all[d] + s_im * g_turned[d] for d in range(chans)]
            parts = [made[d][4 * (t % 2) : 4 * (t % 2) + 4] for d in range(chans)]
            tile = jnp.concatenate(parts, axis=0)
            tiles.append(jnp.where(ch * 16 + i < reads, tile, 0.0))
        for b in range(4):
            low = jnp.zeros((16, LANES), jnp.float32)
            for t in range(4):
                shift = 32 * ((t - b) % 4)
                moved = pltpu.roll(tiles[t], shift, 1) if shift else tiles[t]
                low = jnp.where(lane16 // 32 == t, moved, low)
            zs[pl.ds(b, 16, stride=4), :] = low
        back_rows = zs[...].T
        for t in range(4):
            for p in range(2):
                at = 32 * t + 16 * p
                sgv[2 * pair + t // 2, pl.ds(2 * p + t % 2, 16, stride=4), :] = back_rows[at : at + 16]
        return carry

    lax.fori_loop(0, 8, weights_out, 0)
    sgrad_copy = pltpu.make_async_copy(sgv, sgrad_hbm, osem.at[1])
    sgrad_copy.start()

    wait_bytes(red_all.at[pl.ds(1, slabs - 1)], srecv.at[4])
    total = red_pair[2]
    for j in range(1, slabs):
        total = total + red_all[j]
    gate_ref[...] = total[0:1, :16]
    bgrad_ref[...] = total[1:2, :16]

    wait_bytes(ov, osem.at[0])
    rows_back(1)

    def last_chunk(a, carry):
        branch = column_back(1, a)
        for b in range(4):
            c = 4 * a + b
            here = pl.ds(c * rows, rows)
            ov[here, :] = branch[b * rows : (b + 1) * rows] + gain[c] * gv[here, :]
        here = pl.ds(a * chunk, chunk)
        pltpu.make_async_copy(ov.at[here, :], fgrad_hbm.at[here, :], osem.at[2]).start()
        return carry

    lax.fori_loop(0, 4, last_chunk, 0)
    sgrad_copy.wait()
    for turn in range(2):
        wait_bytes(tx_rows.at[turn, pl.ds(1, slabs - 1)], ssend.at[turn])
        wait_bytes(rx_modes.at[turn, pl.ds(1, slabs - 1)], ssend.at[2 + turn])
        wait_bytes(rx_chan, csend.at[turn])
    wait_bytes(red_all.at[pl.ds(1, slabs - 1)], ssend.at[4])
    wait_bytes(ov, osem.at[2])


def local(source_field, cotangent, spectral_weight, skip_gain, channel_bias, mode_limit, width_limit):
    channels, rows, cols = source_field.shape
    slabs, chans, modes = lax.axis_size("slab"), lax.axis_size("chan"), lax.axis_size("mode")
    outs = spectral_weight.shape[1]
    assert (channels, rows, modes, outs) == (16, 32, 2, 16 * chans)
    assert spectral_weight.shape[2:] == (16, 2, 2)
    flat = (channels * rows, cols)
    w = spectral_weight.transpose(0, 2, 3, 4, 1).reshape(channels, 64, outs)
    f32, bf16 = jnp.float32, jnp.bfloat16
    vmem = pltpu.VMEM
    any_space = pl.BlockSpec(memory_space=pl.ANY)
    smem = pl.BlockSpec(memory_space=pltpu.SMEM)
    row = pl.BlockSpec(memory_space=pltpu.VMEM)
    square = (LANES, LANES)
    out, fgrad, sgrad, gate, bgrad = pl.pallas_call(
        functools.partial(kernel, (slabs, chans, modes, rows, cols)),
        out_shape=(
            jax.ShapeDtypeStruct(flat, f32),
            jax.ShapeDtypeStruct(flat, f32),
            jax.ShapeDtypeStruct(w.shape, f32),
            jax.ShapeDtypeStruct((1, channels), f32),
            jax.ShapeDtypeStruct((1, channels), f32),
        ),
        in_specs=[any_space] * 3 + [smem] * 4,
        out_specs=[any_space] * 3 + [row] * 2,
        scratch_shapes=[
            vmem(flat, f32), vmem(flat, f32), vmem(w.shape, f32), vmem(flat, f32), vmem(flat, f32),
            vmem((cols, 2 * LANES), bf16), vmem((cols, 2 * LANES), bf16),
            vmem((2 * LANES, cols), bf16), vmem((2 * LANES, cols), bf16),
            vmem((8 * slabs, 2 * LANES), bf16), vmem((8 * slabs, 2 * LANES), bf16),
            vmem((2 * LANES, 8 * slabs), bf16), vmem((2 * LANES, 8 * slabs), bf16),
            vmem((channels, chans, 8, LANES), f32), vmem((outs, LANES), f32),
            vmem((channels, 2, 8, LANES), f32), vmem(w.shape, f32),
            vmem(square, f32), vmem((2, *square), f32), vmem((2, *square), f32),
            vmem((2, slabs, 8, LANES), f32), vmem((2, slabs, 8, LANES), f32),
            vmem((chans, 8, LANES), f32), vmem((chans - 1, 8, LANES), f32),
            vmem((2, 8, LANES), f32), vmem((2, slabs, 8, LANES), f32),
            vmem((2, *square), f32), vmem((2, *square), f32),
            vmem((chans, 8, LANES), f32), vmem((3, 2, LANES), f32), vmem((slabs, 2, LANES), f32),
            pltpu.SemaphoreType.DMA((3,)), pltpu.SemaphoreType.DMA((3,)),
            pltpu.SemaphoreType.DMA((5,)), pltpu.SemaphoreType.DMA((5,)),
            pltpu.SemaphoreType.DMA((5,)), pltpu.SemaphoreType.DMA((5,)),
            pltpu.SemaphoreType.DMA((2,)), pltpu.SemaphoreType.DMA((2,)),
        ],
        compiler_params=pltpu.CompilerParams(collective_id=0, has_side_effects=True, vmem_limit_bytes=40 << 20),
        name="fno_layer",
    )(
        source_field.reshape(flat), cotangent.reshape(flat), w, skip_gain, channel_bias,
        mode_limit.T, width_limit,
    )
    sgrad = sgrad.reshape(channels, 16, 2, 2, outs).transpose(0, 4, 1, 2, 3)
    return (
        out.reshape(source_field.shape), fgrad.reshape(source_field.shape), sgrad,
        gate.reshape(channels), bgrad.reshape(channels),
    )


def solution(mesh):
    field = P(("member", "chan"), "slab", "mode")
    weight = P(("member", "chan"), None, "mode", None, "slab")
    channel = P(("member", "chan"))
    return jax.shard_map(
        local,
        mesh=mesh,
        in_specs=(field, field, weight, channel, channel, P("member", None), P("member")),
        out_specs=(field, field, weight, channel, channel),
        check_vma=False,
    )
```

time: 278 us -> 145 us (0.52)
  Pallas kernels: 0 us -> 136 us
  waiting for transfers between devices: 94.1 us -> 0 us
  starting transfers between devices: 80.4 us -> 0 us
  blocking collectives: 59.7 us -> 0 us
  matrix products: 17.5 us -> 0 us
  other arithmetic: 10.6 us -> 0 us
  local copies, waits for them, and re-layouts: 13.2 us -> 7.93 us
    pallas_call x0 -> x1, Pallas kernels: none -> 136 us  [local(): pl.pallas_call(functools.partial(kernel, (slabs, chans, modes, rows, cols...]
    all_to_all x6 -> x0, waiting for transfers between devices: 94.1 us -> none  [the longest x4 61.9 us: sum_at_owner(): lax.all_to_all(tiles, axis, split_axis=0, concat_axis=0, tiled=True)]
    all_to_all x6 -> x0, starting transfers between devices: 80.4 us -> none  [the longest x4 59.4 us: sum_at_owner(): lax.all_to_all(tiles, axis, split_axis=0, concat_axis=0, tiled=True)]
    all_to_all x2 -> x0, blocking collectives: 34 us -> none  [the longest x1 30.2 us: from_everyone(): return lax.all_to_all(copies, axis, split_axis=0, concat_axis=0, tiled=True)]
    all_gather x3 -> x0, blocking collectives: 25.7 us -> none  [the longest x2 15.4 us: synthesis(): gathered = lax.all_gather(rebuilt, 'mode', axis=1, tiled=True)]
    dot_general x24 -> x0, matrix products: 17.5 us -> none  [the longest x2 6.39 us: synthesis(): return jnp.einsum('ckh,wk->chw', gathered, column_tab, precision=precise)]
    all_to_all x5 -> x0, other arithmetic: 4.86 us -> none  [the longest x3 2.87 us: sum_at_owner(): lax.all_to_all(tiles, axis, split_axis=0, concat_axis=0, tiled=True)]
    unnamed x27 -> x19, local copies, waits for them, and re-layouts: 5.86 us -> 7.93 us
  transfers between devices with their start and end apart: 6 -> 0, of which waited for: 6 -> 0; matrix products, arithmetic and copies ran while one was open for 3% -> 0% of each run, Pallas kernels for 0% -> 0%
where the time goes in v1:
time: 145 us
  Pallas kernels  136 us (94%)
  local copies, waits for them, and re-layouts  7.93 us (5%)
    pallas_call x1, Pallas kernels, local(): pl.pallas_call(functools.partial(kernel, (slabs, chans, modes, rows, cols...  136 us
    unnamed x19, local copies, waits for them, and re-layouts  7.93 us

profile of v1, /device:TPU:33, one launch (start us, length us, event | category | flops | bytes accessed | tf_op | source)
XLA Modules:
  0.0 144.6 jit_solution(4930782859146088015)
XLA Ops:
  0.6 0.0 copy-start.5
  0.6 0.0 copy-start.6
  0.7 0.0 copy-start.3
  0.7 0.0 copy-start.4
  0.7 0.6 copy-done.5
  1.3 0.0 copy-done.6
  1.3 0.0 copy-done.3
  1.3 0.0 copy-done.4
  1.3 0.0 copy-start
  1.4 1.2 copy-done
  2.6 0.0 copy-start.1
  2.6 1.2 copy-done.1
  3.8 0.0 copy-start.2
  3.8 1.0 copy-done.2
  4.8 136.0 %fno_layer.1 = (f32[512,512]{1,0:T(8,128)S(1)}, f32[512,512]{1,0:T(8,128)S(1)}, f32[16,64,64]{2,1,0:T(8,128)S(1)}, f32[1,16]{1,0:T(1,128)S(1)}, f32[1,16]{1,0:T(1,128)S(1)}) custom-call(f32[512,512]{1,0:T(8,128)S(1)} %bitcast.13, f32[512,512]{1,0:T(8,128)S(1)} %bitcast.14, f32[16,64,64]{2,1,0:T(8,128)S(1)} %bitcast.17, f32[16]{0:T(128)S(1)} %copy-done.4, ...), custom_call_target="tpu_custom_call" | custom-call | tf_op jit(solution)/shard_map/fno_layer/pallas_call | solution.py:417
  140.8 1.0 copy.17
  141.8 1.0 copy.18
  142.8 0.8 copy.19
  143.6 0.5 copy.20
  144.1 0.5 copy.21
Async XLA Ops:
  0.6 0.7 copy-start.5
  0.6 0.7 copy-start.6
  0.7 0.7 copy-start.3
  0.7 0.7 copy-start.4
  1.3 1.2 copy-start
  2.6 1.2 copy-start.1
  3.8 1.0 copy-start.2

commit v2 on v1

v2 whole, which is shorter than its diff:
```python
import functools
import math

import jax
import jax.numpy as jnp
from jax import lax
from jax.experimental import pallas as pl
from jax.experimental.pallas import tpu as pltpu
from jax.sharding import PartitionSpec as P

MESH = pl.DeviceIdType.MESH
LANES = 128
GELU_SLOPE = math.sqrt(2.0 / math.pi)
GELU_CUBE = 0.044715


def slab_offsets(slabs):
    hubs = slabs // 8 - 1
    far = [4 * m for m in range(1, hubs + 1)]
    found = [0, slabs // 2] + far + [-k for k in far]
    for sign in (1, -1):
        for j in range(1, 4):
            found += [sign * (j + 4 * m) for m in range(hubs + 1)]
    return found


def offset_of(slot, slabs):
    hubs = slabs // 8 - 1
    first = 2 + 2 * hubs
    near = jnp.where(slot < 2 + hubs, 4 * (slot - 1), -4 * (slot - 1 - hubs))
    group, m = (slot - first) // (hubs + 1), (slot - first) % (hubs + 1)
    behind = jnp.where(group < 3, 1 + group + 4 * m, -(group - 2) - 4 * m)
    found = jnp.where(slot < first, near, behind)
    return jnp.where(slot == 0, 0, jnp.where(slot == 1, slabs // 2, found))


def split(x):
    high = x.astype(jnp.bfloat16)
    low = (x - high.astype(jnp.float32)).astype(jnp.bfloat16)
    return high, low


def dot3(a, b):
    (ah, al), (bh, bl) = a, b
    dot = functools.partial(jnp.dot, preferred_element_type=jnp.float32)
    return dot(ah, bh) + (dot(ah, bl) + dot(al, bh))


def sine(turns, extent):
    half, quarter = extent // 2, extent // 4
    t = ((turns + half) & (extent - 1)) - half
    t = jnp.where(t > quarter, half - t, jnp.where(t < -quarter, -half - t, t))
    v = t.astype(jnp.float32) * (2.0 * math.pi / extent)
    s = v * v
    poly = -2.5052108e-8
    for c in (2.7557319e-6, -1.9841270e-4, 8.3333333e-3, -1.6666667e-1, 1.0):
        poly = poly * s + c
    return poly * v


def iota(shape, dim):
    return lax.broadcasted_iota(jnp.int32, shape, dim)


def kernel(
    dims,
    x_hbm, cot_hbm, w_hbm, gain_hbm, bias_hbm, limit_hbm, width_hbm,
    ov, gv, sgv, gate_ref, bgrad_ref, last_own, last_rx, tth, ttl,
    xv, cv, wv, gain, bias, limit, width, tch, tcl, fh, fl, fth, ftl,
    wt, zs, sv,
    own_cols, tx_cols, rx_cols, tx_rows, rx_near, rx_anti, tx_far, rx_far, tx_chan, rx_chan, rx_modes,
    own_g, rx_g, g_chan, red_pair, red_near, red_far,
    lsem, msend, mrecv, ssend, nrecv, frecv, hrecv, arecv, csend, crecv, rsend, rrecv,
):
    slabs, chans, modes, rows, cols = dims
    chunk = 4 * rows
    me, ch, mo = lax.axis_index("slab"), lax.axis_index("chan"), lax.axis_index("mode")
    other = 1 - mo
    all_rows, all_cols = slabs * rows, modes * cols
    kx_count = 2 * slabs

    scope = jax.named_scope
    barrier = pltpu.get_barrier_semaphore()

    hubs = slabs // 8 - 1
    offsets = slab_offsets(slabs)
    partners = [k for k in offsets if k and (k % 4 == 0 or abs(k) < 4) and k != slabs // 2]

    def slab_at(k):
        return {"slab": (me + k + slabs) & (slabs - 1)}

    with scope("greet"):
        for k in partners:
            pl.semaphore_signal(barrier, inc=1, device_id=slab_at(k), device_id_type=MESH)
    for k in range(1, chans):
        pl.semaphore_signal(barrier, inc=1, device_id={"chan": lax.rem(ch + k, chans)}, device_id_type=MESH)
    pl.semaphore_signal(barrier, inc=1, device_id={"mode": other}, device_id_type=MESH)

    pairs = (
        (x_hbm, xv), (cot_hbm, cv), (w_hbm, wv), (limit_hbm, limit), (width_hbm, width),
        (gain_hbm, gain), (bias_hbm, bias),
    )
    loads = [pltpu.make_async_copy(a, b, lsem.at[n]) for n, (a, b) in enumerate(pairs)]
    for load in loads:
        load.start()
    def to_mode(slot, src, dst):
        return pltpu.make_async_remote_copy(
            src_ref=src, dst_ref=dst, send_sem=msend.at[slot], recv_sem=mrecv.at[slot],
            device_id={"mode": other}, device_id_type=MESH,
        )

    def to_slab(k, src, dst, send_sem, recv_sem):
        pltpu.make_async_remote_copy(
            src_ref=src, dst_ref=dst, send_sem=send_sem, recv_sem=recv_sem,
            device_id=slab_at(k), device_id_type=MESH,
        ).start()

    def wait_bytes(ref, sem):
        pltpu.make_async_copy(ref, ref, sem).wait()

    lane = iota((8, LANES), 1)
    real_part = lane % 32 < 16

    def turned(v):
        re = iota(v.shape, 1) & 31 < 16
        return jnp.where(re, pltpu.roll(v, LANES - 16, 1), -pltpu.roll(v, 16, 1))

    def column_angles(n, w):
        holder = jnp.where(n < LANES, mo, other)
        freq = holder * 16 + (n & 15)
        cell = mo * cols + w
        return freq * cell + jnp.where(n & 31 < 16, all_cols // 4, all_cols // 2)

    with scope("column_table"):
        shape = (cols, 2 * LANES)
        tch[...], tcl[...] = split(sine(column_angles(iota(shape, 1), iota(shape, 0)), all_cols))

    def row_angles(k, n):
        kx = 2 * ((me + offset_of(k >> 3, slabs) + slabs) & (slabs - 1)) + ((k >> 2) & 1)
        kx = jnp.where(kx < kx_count // 2, kx, kx + all_rows - kx_count)
        half = LANES
        cell = me * rows + (n & (rows - 1))
        angle = kx * cell + jnp.where(n < half, all_rows // 4, 0)
        same = (k & 3) == ((n & (half - 1)) // rows)
        return jnp.where(same, sine(angle, all_rows), 0.0)

    def column_forward(a, values):
        d = dot3(split(values), (tch[...], tcl[...]))
        block = (iota((rows, 2 * LANES), 1) % LANES) // 32
        packed = d[:rows]
        for b in range(1, 4):
            packed = jnp.where(block == b, d[b * rows : (b + 1) * rows], packed)
        own_cols[pl.ds(a * rows, rows), :] = packed[:, :LANES]
        return packed[:, LANES:]

    with scope("load_wait"):
        loads[0].wait()

    def first_chunk(a, carry):
        values = xv[pl.ds(a * chunk, chunk), :]
        tx_cols[0, pl.ds(a * rows, rows), :] = column_forward(a, values)
        return carry

    with scope("first_columns"):
        lax.fori_loop(0, 4, first_chunk, 0)
    with scope("barrier_wait"):
        pl.semaphore_wait(barrier, len(partners) + chans - 1 + 1)

    def rows_forward(turn):
        copy = to_mode(turn, tx_cols.at[turn], rx_cols.at[turn])
        copy.start()
        if turn == 0:
            with scope("row_table"):
                shape = (8 * slabs, 2 * LANES)
                fh[...], fl[...] = split(row_angles(iota(shape, 0), iota(shape, 1)))
        with scope("columns_pair"):
            copy.wait()
        with scope("rows_dot"):
            lined = own_cols[...] + rx_cols[turn]
            both = jnp.concatenate([lined, turned(lined)], axis=0)
            partial = dot3((fh[...], fl[...]), split(both))
            tx_rows[turn] = partial.reshape(slabs, 8, LANES)
        with scope("rows_send"):
            for m in range(hubs, -1, -1):
                if m == hubs:
                    to_slab(4, tx_rows.at[turn, 1], rx_anti.at[turn], ssend.at[turn, 0], nrecv.at[turn, 2, 0])
                for j in (3, 2, 1):
                    for side in range(2):
                        slot = 2 + 2 * hubs + (3 * side + j - 1) * (hubs + 1) + m
                        to_slab(
                            j if side == 0 else -j, tx_rows.at[turn, slot], rx_near.at[turn, side, m, j - 1],
                            ssend.at[turn, 1], nrecv.at[turn, side, m],
                        )

    def owned(turn):
        for m in range(hubs, 0, -1):
            for side in range(2):
                with scope("near_wait"):
                    wait_bytes(rx_near.at[turn, side, m], nrecv.at[turn, side, m])
                slot = 1 + hubs * side + m
                total = tx_rows[turn, slot]
                for j in range(3):
                    total = total + rx_near[turn, side, m, j]
                if m == hubs and side == 0:
                    wait_bytes(rx_anti.at[turn], nrecv.at[turn, 2, 0])
                    total = total + rx_anti[turn]
                tx_far[turn, slot - 2] = total
                to_slab(
                    4 * m if side == 0 else -4 * m, tx_far.at[turn, slot - 2], rx_far.at[turn, slot - 2],
                    ssend.at[turn, 2], frecv.at[turn],
                )
        total = tx_rows[turn, 0]
        for side in range(2):
            wait_bytes(rx_near.at[turn, side, 0], nrecv.at[turn, side, 0])
            for j in range(3):
                total = total + rx_near[turn, side, 0, j]
        with scope("rows_wait"):
            wait_bytes(rx_far.at[turn], frecv.at[turn])
        for n in range(2 * hubs):
            total = total + rx_far[turn, n]
        return total

    rows_forward(0)

    with scope("back_tables"):
        shape = (2 * LANES, cols)
        tth[...], ttl[...] = split(sine(column_angles(iota(shape, 0), iota(shape, 1)), all_cols))
        shape = (2 * LANES, 8 * slabs)
        fth[...], ftl[...] = split(row_angles(iota(shape, 1), iota(shape, 0)))

    for load in loads[3:]:
        load.wait()
    sub = iota((8, LANES), 0)
    keep_col = jnp.zeros((8, LANES), jnp.int32)
    keep_row = jnp.zeros((8, LANES), jnp.int32)
    for c in range(16):
        here = (sub % 4 == c // 4) & (lane // 32 == c % 4)
        keep_col = jnp.where(here, limit[0, ch * 16 + c], keep_col)
        keep_row = jnp.where(here, limit[1, ch * 16 + c], keep_row)
    col_freq = mo * 16 + lane % 16
    row_freq = me * 2 + sub // 4
    kept = (col_freq < keep_col) & ((row_freq < keep_row) | (kx_count - row_freq < keep_row))
    scale = jnp.where(col_freq == 0, 1.0, 2.0) / (all_rows * all_cols)
    weights = jnp.where(kept, scale, 0.0)

    sub16 = iota((16, LANES), 0)
    lane16 = iota((16, LANES), 1)
    reads = jnp.zeros((16, LANES), jnp.int32)
    for o in range(16 * chans):
        reads = jnp.where((sub16 == o // 4) & (lane16 // 32 == o % 4), width[o], reads)

    loads[2].wait()

    def weights_in(pair, carry):
        parts = []
        for t in range(4):
            for p in range(2):
                parts.append(wv[2 * pair + t // 2, pl.ds(2 * p + t % 2, 16, stride=4), :])
        zs[...] = jnp.concatenate(parts, axis=0).T
        by_low = [zs[pl.ds(b, 16, stride=4), :] for b in range(4)]
        for t in range(4):
            i = 2 * pair + t // 2
            tile = jnp.zeros((16, LANES), jnp.float32)
            for b in range(4):
                shift = 32 * ((b - t) % 4)
                moved = pltpu.roll(by_low[b], shift, 1) if shift else by_low[b]
                tile = jnp.where(lane16 // 32 == b, moved, tile)
            tile = jnp.where(ch * 16 + i < reads, tile, 0.0)
            for d in range(chans):
                wt[i, d, pl.ds(4 * (t % 2), 4), :] = tile[4 * d : 4 * d + 4]
        return carry

    with jax.named_scope("weights_in"):
        lax.fori_loop(0, 8, weights_in, 0)

    spectra = owned(0)
    for a in range(4):
        e = jnp.where(
            sub < 4,
            jnp.broadcast_to(spectra[a : a + 1], (8, LANES)),
            jnp.broadcast_to(spectra[4 + a : 5 + a], (8, LANES)),
        )
        rolled = [e] + [pltpu.roll(e, 16 * m, 1) for m in range(1, 8)]
        for q in range(8):
            copies = rolled[(0 - q) % 8]
            for t in range(1, 8):
                copies = jnp.where(lane // 16 == t, rolled[(t - q) % 8], copies)
            sv[4 * a + q // 2, q % 2] = copies

    zero = jnp.zeros((8, LANES), jnp.float32)

    def contract(i, sums):
        s_re, s_im = sv[i, 0], sv[i, 1]
        first = tuple(sums[d] + s_re * wt[i, d] for d in range(chans))
        second = tuple(sums[chans + d] + s_im * wt[i, d] for d in range(chans))
        return first + second

    sums = lax.fori_loop(0, 16, contract, (zero,) * (2 * chans), unroll=4)
    for d in range(chans):
        tx_chan[d] = sums[d] - turned(sums[chans + d])

    def to_chan(slot, k, src, dst):
        return pltpu.make_async_remote_copy(
            src_ref=src, dst_ref=dst, send_sem=csend.at[slot], recv_sem=crecv.at[slot],
            device_id={"chan": lax.rem(ch + k, chans)}, device_id_type=MESH,
        )

    for k in range(1, chans):
        to_chan(0, k, tx_chan.at[lax.rem(ch + k, chans)], rx_chan.at[chans - 1 - k]).start()
    with scope("chan_wait"):
        wait_bytes(rx_chan, crecv.at[0])
    modes_out = tx_chan[ch]
    for k in range(chans - 1):
        modes_out = modes_out + rx_chan[k]

    def everywhere(turn, tile):
        rx = rx_modes.at[turn]
        rx[0] = tile
        with scope("modes_send"):
            for m in range(hubs, 0, -1):
                for side, k in enumerate((4 * m, -4 * m)):
                    to_slab(
                        k, rx.at[0], rx.at[offsets.index(-k)], ssend.at[2 + turn, 0], hrecv.at[turn, m - 1, side]
                    )
            for j in (3, 2, 1):
                for k in (j, -j):
                    to_slab(k, rx.at[0], rx.at[offsets.index(-k)], ssend.at[2 + turn, 0], arecv.at[turn])

    def passed_on(turn):
        rx = rx_modes.at[turn]
        for m in range(1, hubs + 1):
            for side in range(2):
                sign = 1 if side == 0 else -1
                held = rx.at[offsets.index(-sign * 4 * m)]
                with scope("hub_wait"):
                    wait_bytes(held, hrecv.at[turn, m - 1, side])
                for j in (4, 3, 2, 1) if m == hubs and side == 0 else (3, 2, 1):
                    there = rx.at[1 if j == 4 else offsets.index(-sign * (4 * m + j))]
                    to_slab(sign * j, held, there, ssend.at[2 + turn, 1], arecv.at[turn])

    def rows_back(turn):
        with scope("modes_wait"):
            wait_bytes(rx_modes.at[turn, pl.ds(0, slabs - 1 - 2 * hubs)], arecv.at[turn])
        with scope("back_dot"):
            found = rx_modes[turn].reshape(8 * slabs, LANES)
            both = dot3((fth[...], ftl[...]), split(found))
            own_g[turn] = both[:LANES] - turned(both[LANES:])
        with scope("back_pair"):
            copy = to_mode(2 + turn, own_g.at[turn], rx_g.at[turn])
            copy.start()
            copy.wait()

    everywhere(0, modes_out * weights)
    loads[1].wait()
    passed_on(0)
    rows_back(0)

    def gelu_chunk(a, carry):
        gates, biases = carry
        branch = column_synthesis(own_g.at[0], rx_g.at[0], a, rows, (tth, ttl))
        grads = []
        for b in range(4):
            c = 4 * a + b
            here = pl.ds(c * rows, rows)
            x = xv[here, :]
            v = branch[b * rows : (b + 1) * rows] + gain[c] * x + bias[c]
            v2 = v * v
            t = jnp.tanh(GELU_SLOPE * (v + GELU_CUBE * (v2 * v)))
            cdf = 0.5 * (1.0 + t)
            ov[here, :] = v * cdf
            slope = cdf + (0.5 * GELU_SLOPE) * (v * (1.0 - t * t)) * (1.0 + (3.0 * GELU_CUBE) * v2)
            grad = cv[here, :] * slope
            gv[here, :] = gain[c] * grad
            grads.append(grad)
            gate = jnp.sum(jnp.sum(grad * x, axis=0, keepdims=True), axis=1, keepdims=True)
            plain = jnp.sum(jnp.sum(grad, axis=0, keepdims=True), axis=1, keepdims=True)
            spot = iota((1, LANES), 1) == c
            gates = jnp.where(spot, gate, gates)
            biases = jnp.where(spot, plain, biases)
        tx_cols[1, pl.ds(a * rows, rows), :] = column_forward(a, jnp.concatenate(grads, axis=0))
        return gates, biases

    empty = jnp.zeros((1, LANES), jnp.float32)
    with scope("gelu"):
        gates, biases = lax.fori_loop(0, 4, gelu_chunk, (empty, empty))
    rows_forward(1)

    red_pair[0] = jnp.concatenate([gates, biases], axis=0)
    with scope("pair_sums"):
        copy = to_mode(4, red_pair.at[0], red_pair.at[1])
        copy.start()
        copy.wait()
        red_pair[2] = red_pair[0] + red_pair[1]
        for j in range(1, 4):
            pltpu.make_async_remote_copy(
                src_ref=red_pair.at[2], dst_ref=red_near.at[j - 1], send_sem=rsend.at[0], recv_sem=rrecv.at[0],
                device_id={"slab": me ^ j}, device_id_type=MESH,
            ).start()

    g_chan[ch] = owned(1) * weights
    for k in range(1, chans):
        to_chan(1, k, g_chan.at[ch], g_chan.at[ch]).start()
    with scope("chan_wait_two"):
        wait_bytes(g_chan.at[pl.ds(0, chans - 1)], crecv.at[1])
    g_all = [g_chan[d] for d in range(chans)]
    g_turned = [turned(g) for g in g_all]

    def contract_back(i):
        first, second = zero, zero
        for d in range(chans):
            w = wt[i, d]
            first = first + w * g_all[d]
            second = second + w * g_turned[d]
        v = jnp.where(real_part, first + pltpu.roll(first, 16, 1), second + pltpu.roll(second, 16, 1))
        v = v + pltpu.roll(v, 32, 1)
        return v + pltpu.roll(v, 64, 1)

    back = zero
    for a in range(4):
        m = contract_back(4 * a)
        for b in range(1, 4):
            m = jnp.where(lane // 32 == b, contract_back(4 * a + b), m)
        for x in range(2):
            row = jnp.sum(m[4 * x : 4 * x + 4], axis=0, keepdims=True)
            back = jnp.where(sub == 4 * x + a, jnp.broadcast_to(row, (8, LANES)), back)
    everywhere(1, back)

    with scope("sums_near"):
        wait_bytes(red_near, rrecv.at[0])
        total = red_pair[2]
        for j in range(3):
            total = total + red_near[j]
        red_pair[3] = total
        for m in range(1, hubs + 1):
            for side, k in enumerate((4 * m, -4 * m)):
                last = side * m == hubs
                to_slab(k, red_pair.at[3], red_far.at[hubs * side + m - 1], rsend.at[1], rrecv.at[2 if last else 1])

    def weights_out(pair, carry):
        tiles = []
        for t in range(4):
            i = 2 * pair + t // 2
            if t % 2 == 0:
                s_re, s_im = sv[i, 0], sv[i, 1]
                made = [s_re * g_all[d] + s_im * g_turned[d] for d in range(chans)]
            parts = [made[d][4 * (t % 2) : 4 * (t % 2) + 4] for d in range(chans)]
            tile = jnp.concatenate(parts, axis=0)
            tiles.append(jnp.where(ch * 16 + i < reads, tile, 0.0))
        for b in range(4):
            low = jnp.zeros((16, LANES), jnp.float32)
            for t in range(4):
                shift = 32 * ((t - b) % 4)
                moved = pltpu.roll(tiles[t], shift, 1) if shift else tiles[t]
                low = jnp.where(lane16 // 32 == t, moved, low)
            zs[pl.ds(b, 16, stride=4), :] = low
        back_rows = zs[...].T
        for t in range(4):
            for p in range(2):
                at = 32 * t + 16 * p
                sgv[2 * pair + t // 2, pl.ds(2 * p + t % 2, 16, stride=4), :] = back_rows[at : at + 16]
        return carry

    with scope("weights_out"):
        lax.fori_loop(0, 8, weights_out, 0)
    passed_on(1)
    wait_bytes(red_far.at[2 * hubs - 1], rrecv.at[2])
    to_slab(-4, red_far.at[2 * hubs - 1], red_far.at[2 * hubs], rsend.at[1], rrecv.at[1])
    rows_back(1)
    last_own[...] = own_g[1]
    last_rx[...] = rx_g[1]
    wait_bytes(red_far.at[pl.ds(0, 2 * hubs)], rrecv.at[1])
    total = red_pair[3]
    for m in range(slabs // 4 - 1):
        total = total + red_far[m]
    gate_ref[...] = total[0:1, :16]
    bgrad_ref[...] = total[1:2, :16]
    for turn in range(2):
        wait_bytes(rx_anti.at[turn], ssend.at[turn, 0])
        wait_bytes(rx_near.at[turn], ssend.at[turn, 1])
        wait_bytes(tx_far.at[turn], ssend.at[turn, 2])
        wait_bytes(rx_modes.at[turn, pl.ds(0, 6 + 2 * hubs)], ssend.at[2 + turn, 0])
        wait_bytes(rx_modes.at[turn, pl.ds(0, 6 * hubs + 1)], ssend.at[2 + turn, 1])
        wait_bytes(rx_chan, csend.at[turn])
    wait_bytes(red_near, rsend.at[0])
    wait_bytes(red_far, rsend.at[1])


def column_synthesis(own, theirs, a, rows, tables):
    here = pl.ds(a * rows, rows)
    g = jnp.concatenate([own[here, :], theirs[here, :]], axis=1)
    block = (iota(g.shape, 1) & (LANES - 1)) // 32
    spread = jnp.concatenate([jnp.where(block == b, g, 0.0) for b in range(4)], axis=0)
    return dot3(split(spread), (tables[0][...], tables[1][...]))


def finish(
    rows, ov, gv, sgv, gate, bgrad, own, theirs, tth, ttl,
    out_hbm, fgrad_hbm, sgrad_hbm, gate_hbm, bgrad_hbm,
    fv, sem, fsem,
):
    pairs = ((ov, out_hbm), (sgv, sgrad_hbm), (gate, gate_hbm), (bgrad, bgrad_hbm))
    copies = [pltpu.make_async_copy(a, b, sem.at[n]) for n, (a, b) in enumerate(pairs)]
    for copy in copies:
        copy.start()
    chunk = 4 * rows
    for a in range(4):
        here = pl.ds(a * chunk, chunk)
        fv[here, :] = column_synthesis(own, theirs, a, rows, (tth, ttl)) + gv[here, :]
        copies.append(pltpu.make_async_copy(fv.at[here, :], fgrad_hbm.at[here, :], fsem.at[a]))
        copies[-1].start()
    for copy in copies:
        copy.wait()


def local(source_field, cotangent, spectral_weight, skip_gain, channel_bias, mode_limit, width_limit):
    channels, rows, cols = source_field.shape
    slabs, chans, modes = lax.axis_size("slab"), lax.axis_size("chan"), lax.axis_size("mode")
    outs = spectral_weight.shape[1]
    assert (channels, rows, modes, outs) == (16, 32, 2, 16 * chans)
    assert spectral_weight.shape[2:] == (16, 2, 2)
    flat = (channels * rows, cols)
    w = spectral_weight.transpose(0, 2, 3, 4, 1).reshape(channels, 64, outs)
    limits = mode_limit.T
    f32, bf16 = jnp.float32, jnp.bfloat16
    vmem, sems = pltpu.VMEM, pltpu.SemaphoreType.DMA
    hubs = slabs // 8 - 1
    assert slabs == 8 * (hubs + 1) and hubs > 0
    hbm_spec = pl.BlockSpec(memory_space=pltpu.HBM)
    vmem_spec = pl.BlockSpec(memory_space=pltpu.VMEM)
    square = (LANES, LANES)
    held = (
        (flat, f32), (flat, f32), (w.shape, f32), ((1, channels), f32), ((1, channels), f32),
        (square, f32), (square, f32), ((2 * LANES, cols), bf16), ((2 * LANES, cols), bf16),
    )
    found = pl.pallas_call(
        functools.partial(kernel, (slabs, chans, modes, rows, cols)),
        out_shape=tuple(jax.ShapeDtypeStruct(*h) for h in held),
        in_specs=[hbm_spec] * 7,
        out_specs=[vmem_spec] * len(held),
        scratch_shapes=[
            vmem(flat, f32), vmem(flat, f32), vmem(w.shape, f32),
            pltpu.SMEM(skip_gain.shape, f32), pltpu.SMEM(channel_bias.shape, f32),
            pltpu.SMEM(limits.shape, jnp.int32), pltpu.SMEM(width_limit.shape, jnp.int32),
            vmem((cols, 2 * LANES), bf16), vmem((cols, 2 * LANES), bf16),
            vmem((8 * slabs, 2 * LANES), bf16), vmem((8 * slabs, 2 * LANES), bf16),
            vmem((2 * LANES, 8 * slabs), bf16), vmem((2 * LANES, 8 * slabs), bf16),
            vmem((channels, chans, 8, LANES), f32), vmem((outs, LANES), f32),
            vmem((channels, 2, 8, LANES), f32),
            vmem(square, f32), vmem((2, *square), f32), vmem((2, *square), f32),
            vmem((2, slabs, 8, LANES), f32), vmem((2, 2, hubs + 1, 3, 8, LANES), f32),
            vmem((2, 8, LANES), f32),
            vmem((2, 2 * hubs, 8, LANES), f32), vmem((2, 2 * hubs, 8, LANES), f32),
            vmem((chans, 8, LANES), f32), vmem((chans - 1, 8, LANES), f32),
            vmem((2, slabs, 8, LANES), f32),
            vmem((2, *square), f32), vmem((2, *square), f32),
            vmem((chans, 8, LANES), f32), vmem((4, 2, LANES), f32),
            vmem((3, 2, LANES), f32), vmem((slabs // 4 - 1, 2, LANES), f32),
            sems((7,)), sems((5,)), sems((5,)), sems((4, 3)), sems((2, 3, hubs + 1)), sems((2,)),
            sems((2, hubs, 2)), sems((2,)), sems((2,)), sems((2,)), sems((2,)), sems((3,)),
        ],
        compiler_params=pltpu.CompilerParams(collective_id=0, has_side_effects=True, vmem_limit_bytes=40 << 20),
        name="fno_layer",
    )(
        *(
            pltpu.with_memory_space_constraint(a, pltpu.HBM)
            for a in (
                source_field.reshape(flat), cotangent.reshape(flat), w, skip_gain, channel_bias, limits, width_limit,
            )
        )
    )
    out, fgrad, sgrad, gate, bgrad = pl.pallas_call(
        functools.partial(finish, rows),
        out_shape=tuple(jax.ShapeDtypeStruct(*h) for h in held[:5]),
        in_specs=[vmem_spec] * len(held),
        out_specs=[hbm_spec] * 5,
        scratch_shapes=[vmem(flat, f32), pltpu.SemaphoreType.DMA((4,)), pltpu.SemaphoreType.DMA((4,))],
        compiler_params=pltpu.CompilerParams(vmem_limit_bytes=24 << 20),
        name="fno_finish",
    )(*found)
    sgrad = sgrad.reshape(channels, 16, 2, 2, outs).transpose(0, 4, 1, 2, 3)
    return (
        out.reshape(source_field.shape), fgrad.reshape(source_field.shape), sgrad,
        gate.reshape(channels), bgrad.reshape(channels),
    )


def solution(mesh):
    field = P(("member", "chan"), "slab", "mode")
    weight = P(("member", "chan"), None, "mode", None, "slab")
    channel = P(("member", "chan"))
    return jax.shard_map(
        local,
        mesh=mesh,
        in_specs=(field, field, weight, channel, channel, P("member", None), P("member")),
        out_specs=(field, field, weight, channel, channel),
        check_vma=False,
    )
```

time: 145 us -> 128 us (0.88)
  Pallas kernels: 136 us -> 127 us
  local copies, waits for them, and re-layouts: 7.93 us -> 0 us
    pallas_call x1, Pallas kernels: 136 us -> 125 us  [local(): pl.pallas_call(functools.partial(kernel, (slabs, chans, modes, rows, cols...]
    unnamed x19 -> x0, local copies, waits for them, and re-layouts: 7.93 us -> none
    pallas_call x0 -> x1, Pallas kernels: none -> 1.57 us  [local(): pl.pallas_call(functools.partial(finish, rows), out_shape=tuple((jax.Shap...]
where the time goes in v2:
time: 128 us; the launch traced here: 127 us
  Pallas kernels  127 us (99%)
    pallas_call x1, Pallas kernels, local(): pl.pallas_call(functools.partial(kernel, (slabs, chans, modes, rows, cols...  125 us

profile of v2, /device:TPU:33, one launch (start us, length us, event | category | flops | bytes accessed | tf_op | source)
XLA Modules:
  0.0 127.5 jit_solution(2048414030659599400)
XLA Ops:
  0.6 125.3 %fno_layer.1 = (f32[512,512]{1,0:T(8,128)S(1)}, f32[512,512]{1,0:T(8,128)S(1)}, f32[16,64,64]{2,1,0:T(8,128)S(1)}, f32[1,16]{1,0:T(1,128)S(1)}, f32[1,16]{1,0:T(...) custom-call(f32[512,512]{1,0:T(8,128)} %bitcast.13, ...), custom_call_target="tpu_custom_call" | custom-call | tf_op jit(solution)/shard_map/fno_layer/pallas_call | solution.py:535
  125.9 1.6 %fno_finish.1 = (f32[512,512]{1,0:T(8,128)}, f32[512,512]{1,0:T(8,128)}, f32[16,64,64]{2,1,0:T(8,128)}, f32[1,16]{1,0:T(1,128)}, f32[1,16]{1,0:T(1,128)}) custom-call(f32[512,512]{1,0:T(8,128)S(1)} %get-tuple-element.19.ov, f32[512,512]{1,0:T(8,128)S(1)} %get-tuple-element.20.gv, f32[16,64,64]{2,1,0:T(8,128)S(1)} %get-tuple-element.21.sgv, ...), custom_call_target="tpu_custom_call" | custom-call | tf_op jit(solution)/shard_map/fno_finish/pallas_call | solution.py:571

commit v3 on v2

--- a/solution.py
+++ b/solution.py
@@ -22,6 +22,23 @@
         for j in range(1, 4):
             found += [sign * (j + 4 * m) for m in range(hubs + 1)]
     return found
+
+
+def both_ways(ks):
+    return [sign * k for k in ks for sign in (1, -1)]
+
+
+def early_plan(slabs):
+    top = slabs // 4
+    hubs = [(top, slabs // 2 - top), (-top, slabs // 2 - top - 1), (4, top - 5), (-4, top - 5)]
+    return hubs, [], both_ways((3, 2, 1))
+
+
+def main_plan(slabs):
+    half = slabs // 2
+    hubs = [(k, half // 2 - 4 if abs(k) > 4 else 3) for k in both_ways((half // 2, 4))]
+    first = [half] + both_ways(range(half - 1, half // 2 + half // 2 - 4, -1))
+    return hubs, first, both_ways((3, 2, 1))
 
 
 def offset_of(slot, slabs):
@@ -68,7 +85,7 @@
     ov, gv, sgv, gate_ref, bgrad_ref, last_own, last_rx, tth, ttl,
     xv, cv, wv, gain, bias, limit, width, tch, tcl, fh, fl, fth, ftl,
     wt, zs, sv,
-    own_cols, tx_cols, rx_cols, tx_rows, rx_near, rx_anti, tx_far, rx_far, tx_chan, rx_chan, rx_modes,
+    own_cols, tx_cols, rx_cols, tx_rows, rx_near, tx_far, rx_far, tx_chan, rx_chan, rx_modes,
     own_g, rx_g, g_chan, red_pair, red_near, red_far,
     lsem, msend, mrecv, ssend, nrecv, frecv, hrecv, arecv, csend, crecv, rsend, rrecv,
 ):
@@ -84,7 +101,12 @@
 
     hubs = slabs // 8 - 1
     offsets = slab_offsets(slabs)
-    partners = [k for k in offsets if k and (k % 4 == 0 or abs(k) < 4) and k != slabs // 2]
+    partners = [k for k in offsets if 0 < abs(k) <= slabs // 4]
+    early, main = early_plan(slabs), main_plan(slabs)
+
+    def slot_of(k):
+        k %= slabs
+        return offsets.index(k - slabs if k > slabs // 2 else k)
 
     def slab_at(k):
         return {"slab": (me + k + slabs) & (slabs - 1)}
@@ -153,6 +175,10 @@
         own_cols[pl.ds(a * rows, rows), :] = packed[:, :LANES]
         return packed[:, LANES:]
 
+    with scope("row_table"):
+        shape = (8 * slabs, 2 * LANES)
+        fh[...], fl[...] = split(row_angles(iota(shape, 0), iota(shape, 1)))
+
     with scope("load_wait"):
         loads[0].wait()
 
@@ -162,17 +188,13 @@
         return carry
 
     with scope("first_columns"):
-        lax.fori_loop(0, 4, first_chunk, 0)
+        lax.fori_loop(0, 4, first_chunk, 0, unroll=True)
     with scope("barrier_wait"):
         pl.semaphore_wait(barrier, len(partners) + chans - 1 + 1)
 
     def rows_forward(turn):
         copy = to_mode(turn, tx_cols.at[turn], rx_cols.at[turn])
         copy.start()
-        if turn == 0:
-            with scope("row_table"):
-                shape = (8 * slabs, 2 * LANES)
-                fh[...], fl[...] = split(row_angles(iota(shape, 0), iota(shape, 1)))
         with scope("columns_pair"):
             copy.wait()
         with scope("rows_dot"):
@@ -181,42 +203,52 @@
             partial = dot3((fh[...], fl[...]), split(both))
             tx_rows[turn] = partial.reshape(slabs, 8, LANES)
         with scope("rows_send"):
-            for m in range(hubs, -1, -1):
-                if m == hubs:
-                    to_slab(4, tx_rows.at[turn, 1], rx_anti.at[turn], ssend.at[turn, 0], nrecv.at[turn, 2, 0])
-                for j in (3, 2, 1):
-                    for side in range(2):
-                        slot = 2 + 2 * hubs + (3 * side + j - 1) * (hubs + 1) + m
-                        to_slab(
-                            j if side == 0 else -j, tx_rows.at[turn, slot], rx_near.at[turn, side, m, j - 1],
-                            ssend.at[turn, 1], nrecv.at[turn, side, m],
-                        )
+            chain, first, last = main if turn else early
+
+            def near(n):
+                k, reach = chain[n]
+                for j in range(reach, 0, -1):
+                    step = j if k > 0 else -j
+                    to_slab(
+                        step, tx_rows.at[turn, slot_of(k + step)], rx_near.at[turn, n, j - 1],
+                        ssend.at[turn, 1], nrecv.at[turn, n],
+                    )
+
+            def direct(ks, at):
+                for n, k in enumerate(ks):
+                    to_slab(k, tx_rows.at[turn, slot_of(k)], rx_far.at[turn, at + n], ssend.at[turn, 0], frecv.at[turn])
+
+            near(0)
+            near(1)
+            direct(first, len(chain))
+            for n in range(2, len(chain)):
+                near(n)
+            direct(last, len(chain) + len(first))
 
     def owned(turn):
-        for m in range(hubs, 0, -1):
-            for side in range(2):
-                with scope("near_wait"):
-                    wait_bytes(rx_near.at[turn, side, m], nrecv.at[turn, side, m])
-                slot = 1 + hubs * side + m
-                total = tx_rows[turn, slot]
+        chain, first, last = main if turn else early
+        for n, (k, reach) in enumerate(chain):
+            with scope("near_wait"):
+                wait_bytes(rx_near.at[turn, n, pl.ds(0, reach)], nrecv.at[turn, n])
+            total = tx_rows[turn, slot_of(k)]
+            for j in range(reach):
+                total = total + rx_near[turn, n, j]
+            tx_far[turn, n] = total
+            to_slab(k, tx_far.at[turn, n], rx_far.at[turn, n], ssend.at[turn, 2], frecv.at[turn])
+        if turn:
+            with scope("sums_near"):
+                wait_bytes(red_near, rrecv.at[0])
+                total = red_pair[2]
                 for j in range(3):
-                    total = total + rx_near[turn, side, m, j]
-                if m == hubs and side == 0:
-                    wait_bytes(rx_anti.at[turn], nrecv.at[turn, 2, 0])
-                    total = total + rx_anti[turn]
-                tx_far[turn, slot - 2] = total
-                to_slab(
-                    4 * m if side == 0 else -4 * m, tx_far.at[turn, slot - 2], rx_far.at[turn, slot - 2],
-                    ssend.at[turn, 2], frecv.at[turn],
-                )
+                    total = total + red_near[j]
+                red_pair[3] = total
+                for m in range(1, slabs // 4):
+                    to_slab(4 * m, red_pair.at[3], red_far.at[m - 1], rsend.at[1], rrecv.at[1])
+        count = len(chain) + len(first) + len(last)
+        with scope("rows_wait"):
+            wait_bytes(rx_far.at[turn, pl.ds(0, count)], frecv.at[turn])
         total = tx_rows[turn, 0]
-        for side in range(2):
-            wait_bytes(rx_near.at[turn, side, 0], nrecv.at[turn, side, 0])
-            for j in range(3):
-                total = total + rx_near[turn, side, 0, j]
-        with scope("rows_wait"):
-            wait_bytes(rx_far.at[turn], frecv.at[turn])
-        for n in range(2 * hubs):
+        for n in range(count):
             total = total + rx_far[turn, n]
         return total
 
@@ -317,30 +349,28 @@
         rx = rx_modes.at[turn]
         rx[0] = tile
         with scope("modes_send"):
-            for m in range(hubs, 0, -1):
-                for side, k in enumerate((4 * m, -4 * m)):
-                    to_slab(
-                        k, rx.at[0], rx.at[offsets.index(-k)], ssend.at[2 + turn, 0], hrecv.at[turn, m - 1, side]
-                    )
-            for j in (3, 2, 1):
-                for k in (j, -j):
-                    to_slab(k, rx.at[0], rx.at[offsets.index(-k)], ssend.at[2 + turn, 0], arecv.at[turn])
+            chain, first, last = main
+            order = [k for k, _ in chain[:2]] + first + [k for k, _ in chain[2:]] + last
+            kinds = [k for k, _ in chain]
+            for k in order:
+                sem = hrecv.at[turn, kinds.index(k)] if k in kinds else arecv.at[turn]
+                to_slab(k, rx.at[0], rx.at[slot_of(-k)], ssend.at[2 + turn, 0], sem)
 
     def passed_on(turn):
         rx = rx_modes.at[turn]
-        for m in range(1, hubs + 1):
-            for side in range(2):
-                sign = 1 if side == 0 else -1
-                held = rx.at[offsets.index(-sign * 4 * m)]
-                with scope("hub_wait"):
-                    wait_bytes(held, hrecv.at[turn, m - 1, side])
-                for j in (4, 3, 2, 1) if m == hubs and side == 0 else (3, 2, 1):
-                    there = rx.at[1 if j == 4 else offsets.index(-sign * (4 * m + j))]
-                    to_slab(sign * j, held, there, ssend.at[2 + turn, 1], arecv.at[turn])
+        chain = main[0]
+        for n in list(range(2, len(chain))) + [0, 1]:
+            k, reach = chain[n]
+            held = rx.at[slot_of(-k)]
+            with scope("hub_wait"):
+                wait_bytes(held, hrecv.at[turn, n])
+            for j in range(reach, 0, -1):
+                step = j if k > 0 else -j
+                to_slab(step, held, rx.at[slot_of(-k - step)], ssend.at[2 + turn, 1], arecv.at[turn])
 
     def rows_back(turn):
         with scope("modes_wait"):
-            wait_bytes(rx_modes.at[turn, pl.ds(0, slabs - 1 - 2 * hubs)], arecv.at[turn])
+            wait_bytes(rx_modes.at[turn, pl.ds(0, slabs - 1 - len(main[0]))], arecv.at[turn])
         with scope("back_dot"):
             found = rx_modes[turn].reshape(8 * slabs, LANES)
             both = dot3((fth[...], ftl[...]), split(found))
@@ -382,7 +412,7 @@
 
     empty = jnp.zeros((1, LANES), jnp.float32)
     with scope("gelu"):
-        gates, biases = lax.fori_loop(0, 4, gelu_chunk, (empty, empty))
+        gates, biases = lax.fori_loop(0, 4, gelu_chunk, (empty, empty), unroll=True)
     rows_forward(1)
 
     red_pair[0] = jnp.concatenate([gates, biases], axis=0)
@@ -424,17 +454,6 @@
             row = jnp.sum(m[4 * x : 4 * x + 4], axis=0, keepdims=True)
             back = jnp.where(sub == 4 * x + a, jnp.broadcast_to(row, (8, LANES)), back)
     everywhere(1, back)
-
-    with scope("sums_near"):
-        wait_bytes(red_near, rrecv.at[0])
-        total = red_pair[2]
-        for j in range(3):
-            total = total + red_near[j]
-        red_pair[3] = total
-        for m in range(1, hubs + 1):
-            for side, k in enumerate((4 * m, -4 * m)):
-                last = side * m == hubs
-                to_slab(k, red_pair.at[3], red_far.at[hubs * side + m - 1], rsend.at[1], rrecv.at[2 if last else 1])
 
     def weights_out(pair, carry):
         tiles = []
@@ -463,23 +482,23 @@
     with scope("weights_out"):
         lax.fori_loop(0, 8, weights_out, 0)
     passed_on(1)
-    wait_bytes(red_far.at[2 * hubs - 1], rrecv.at[2])
-    to_slab(-4, red_far.at[2 * hubs - 1], red_far.at[2 * hubs], rsend.at[1], rrecv.at[1])
     rows_back(1)
     last_own[...] = own_g[1]
     last_rx[...] = rx_g[1]
-    wait_bytes(red_far.at[pl.ds(0, 2 * hubs)], rrecv.at[1])
+    wait_bytes(red_far, rrecv.at[1])
     total = red_pair[3]
     for m in range(slabs // 4 - 1):
         total = total + red_far[m]
     gate_ref[...] = total[0:1, :16]
     bgrad_ref[...] = total[1:2, :16]
     for turn in range(2):
-        wait_bytes(rx_anti.at[turn], ssend.at[turn, 0])
-        wait_bytes(rx_near.at[turn], ssend.at[turn, 1])
-        wait_bytes(tx_far.at[turn], ssend.at[turn, 2])
-        wait_bytes(rx_modes.at[turn, pl.ds(0, 6 + 2 * hubs)], ssend.at[2 + turn, 0])
-        wait_bytes(rx_modes.at[turn, pl.ds(0, 6 * hubs + 1)], ssend.at[2 + turn, 1])
+        chain, first, last = main if turn else early
+        wait_bytes(rx_far.at[turn, pl.ds(0, len(first) + len(last))], ssend.at[turn, 0])
+        wait_bytes(tx_rows.at[turn, pl.ds(0, sum(reach for _, reach in chain))], ssend.at[turn, 1])
+        wait_bytes(tx_far.at[turn, pl.ds(0, len(chain))], ssend.at[turn, 2])
+        passed = sum(reach for _, reach in main[0])
+        wait_bytes(rx_modes.at[turn, pl.ds(0, slabs - 1 - passed)], ssend.at[2 + turn, 0])
+        wait_bytes(rx_modes.at[turn, pl.ds(0, passed)], ssend.at[2 + turn, 1])
         wait_bytes(rx_chan, csend.at[turn])
     wait_bytes(red_near, rsend.at[0])
     wait_bytes(red_far, rsend.at[1])
@@ -524,7 +543,11 @@
     f32, bf16 = jnp.float32, jnp.bfloat16
     vmem, sems = pltpu.VMEM, pltpu.SemaphoreType.DMA
     hubs = slabs // 8 - 1
-    assert slabs == 8 * (hubs + 1) and hubs > 0
+    plans = early_plan(slabs), main_plan(slabs)
+    chains = max(len(p[0]) for p in plans)
+    arrivals = max(sum(map(len, p)) for p in plans)
+    reach = max(r for p in plans for _, r in p[0])
+    assert all(sum(r for _, r in p[0]) + sum(map(len, p)) == slabs - 1 for p in plans)
     hbm_spec = pl.BlockSpec(memory_space=pltpu.HBM)
     vmem_spec = pl.BlockSpec(memory_space=pltpu.VMEM)
     square = (LANES, LANES)
@@ -547,16 +570,15 @@
             vmem((channels, chans, 8, LANES), f32), vmem((outs, LANES), f32),
             vmem((channels, 2, 8, LANES), f32),
             vmem(square, f32), vmem((2, *square), f32), vmem((2, *square), f32),
-            vmem((2, slabs, 8, LANES), f32), vmem((2, 2, hubs + 1, 3, 8, LANES), f32),
-            vmem((2, 8, LANES), f32),
-            vmem((2, 2 * hubs, 8, LANES), f32), vmem((2, 2 * hubs, 8, LANES), f32),
+            vmem((2, slabs, 8, LANES), f32), vmem((2, chains, reach, 8, LANES), f32),
+            vmem((2, chains, 8, LANES), f32), vmem((2, arrivals, 8, LANES), f32),
             vmem((chans, 8, LANES), f32), vmem((chans - 1, 8, LANES), f32),
             vmem((2, slabs, 8, LANES), f32),
             vmem((2, *square), f32), vmem((2, *square), f32),
             vmem((chans, 8, LANES), f32), vmem((4, 2, LANES), f32),
             vmem((3, 2, LANES), f32), vmem((slabs // 4 - 1, 2, LANES), f32),
-            sems((7,)), sems((5,)), sems((5,)), sems((4, 3)), sems((2, 3, hubs + 1)), sems((2,)),
-            sems((2, hubs, 2)), sems((2,)), sems((2,)), sems((2,)), sems((2,)), sems((3,)),
+            sems((7,)), sems((5,)), sems((5,)), sems((4, 3)), sems((2, chains)), sems((2,)),
+            sems((2, chains)), sems((2,)), sems((2,)), sems((2,)), sems((2,)), sems((2,)),
         ],
         compiler_params=pltpu.CompilerParams(collective_id=0, has_side_effects=True, vmem_limit_bytes=40 << 20),
         name="fno_layer",

time: 128 us -> 122 us (0.953)
  Pallas kernels: 127 us -> 121 us
    pallas_call x1, Pallas kernels: 125 us -> 119 us  [local(): pl.pallas_call(functools.partial(kernel, (slabs, chans, modes, rows, cols...]
where the time goes in v3:
time: 122 us; the launch traced here: 121 us
  Pallas kernels  121 us (99%)
    pallas_call x1, Pallas kernels, local(): pl.pallas_call(functools.partial(kernel, (slabs, chans, modes, rows, cols...  119 us

profile of v3, /device:TPU:33, one launch (start us, length us, event | category | flops | bytes accessed | tf_op | source)
XLA Modules:
  0.0 121.4 jit_solution(10083818027597430148)
XLA Ops:
  0.6 119.2 %fno_layer.1 = (f32[512,512]{1,0:T(8,128)S(1)}, f32[512,512]{1,0:T(8,128)S(1)}, f32[16,64,64]{2,1,0:T(8,128)S(1)}, f32[1,16]{1,0:T(1,128)S(1)}, f32[1,16]{1,0:T(...) custom-call(f32[512,512]{1,0:T(8,128)} %bitcast.13, ...), custom_call_target="tpu_custom_call" | custom-call | tf_op jit(solution)/shard_map/fno_layer/pallas_call | solution.py:558
  119.8 1.6 %fno_finish.1 = (f32[512,512]{1,0:T(8,128)}, f32[512,512]{1,0:T(8,128)}, f32[16,64,64]{2,1,0:T(8,128)}, f32[1,16]{1,0:T(1,128)}, f32[1,16]{1,0:T(1,128)}) custom-call(f32[512,512]{1,0:T(8,128)S(1)} %get-tuple-element.19.ov, f32[512,512]{1,0:T(8,128)S(1)} %get-tuple-element.20.gv, f32[16,64,64]{2,1,0:T(8,128)S(1)} %get-tuple-element.21.sgv, ...), custom_call_target="tpu_custom_call" | custom-call | tf_op jit(solution)/shard_map/fno_finish/pallas_call | solution.py:593

commit v4 on v3

--- a/solution.py
+++ b/solution.py
@@ -34,11 +34,12 @@
     return hubs, [], both_ways((3, 2, 1))
 
 
-def main_plan(slabs):
+def main_plans(slabs):
     half = slabs // 2
     hubs = [(k, half // 2 - 4 if abs(k) > 4 else 3) for k in both_ways((half // 2, 4))]
-    first = [half] + both_ways(range(half - 1, half // 2 + half // 2 - 4, -1))
-    return hubs, first, both_ways((3, 2, 1))
+    first = [half] + both_ways(range(half - 1, half - 4, -1))
+    many = [(k, 3) for k in both_ways(range(half - 4, 0, -4))]
+    return (hubs, first, both_ways((3, 2, 1))), (many, [half], both_ways((3, 2, 1)))
 
 
 def offset_of(slot, slabs):
@@ -85,7 +86,7 @@
     ov, gv, sgv, gate_ref, bgrad_ref, last_own, last_rx, tth, ttl,
     xv, cv, wv, gain, bias, limit, width, tch, tcl, fh, fl, fth, ftl,
     wt, zs, sv,
-    own_cols, tx_cols, rx_cols, tx_rows, rx_near, tx_far, rx_far, tx_chan, rx_chan, rx_modes,
+    own_cols, tx_cols, rx_cols, tx_rows, rx_near, tx_far, rx_far, tx_chan, rx_chan, rx_modes, mine,
     own_g, rx_g, g_chan, red_pair, red_near, red_far,
     lsem, msend, mrecv, ssend, nrecv, frecv, hrecv, arecv, csend, crecv, rsend, rrecv,
 ):
@@ -101,8 +102,12 @@
 
     hubs = slabs // 8 - 1
     offsets = slab_offsets(slabs)
-    partners = [k for k in offsets if 0 < abs(k) <= slabs // 4]
-    early, main = early_plan(slabs), main_plan(slabs)
+    partners = sorted((k for k in offsets if 0 < abs(k) <= slabs // 4), key=lambda k: -abs(k))
+    early, mains = early_plan(slabs), main_plans(slabs)
+
+    def by_core(f):
+        for core, plan in enumerate(mains):
+            pl.when(mo == core)(functools.partial(f, plan))
 
     def slot_of(k):
         k %= slabs
@@ -202,8 +207,8 @@
             both = jnp.concatenate([lined, turned(lined)], axis=0)
             partial = dot3((fh[...], fl[...]), split(both))
             tx_rows[turn] = partial.reshape(slabs, 8, LANES)
-        with scope("rows_send"):
-            chain, first, last = main if turn else early
+        def send(plan):
+            chain, first, last = plan
 
             def near(n):
                 k, reach = chain[n]
@@ -225,9 +230,11 @@
                 near(n)
             direct(last, len(chain) + len(first))
 
-    def owned(turn):
-        chain, first, last = main if turn else early
-        for n, (k, reach) in enumerate(chain):
+        with scope("rows_send"):
+            by_core(send) if turn else send(early)
+
+    def hub_sums(turn, plan):
+        for n, (k, reach) in enumerate(plan[0]):
             with scope("near_wait"):
                 wait_bytes(rx_near.at[turn, n, pl.ds(0, reach)], nrecv.at[turn, n])
             total = tx_rows[turn, slot_of(k)]
@@ -235,24 +242,27 @@
                 total = total + rx_near[turn, n, j]
             tx_far[turn, n] = total
             to_slab(k, tx_far.at[turn, n], rx_far.at[turn, n], ssend.at[turn, 2], frecv.at[turn])
-        if turn:
-            with scope("sums_near"):
-                wait_bytes(red_near, rrecv.at[0])
-                total = red_pair[2]
-                for j in range(3):
-                    total = total + red_near[j]
-                red_pair[3] = total
-                for m in range(1, slabs // 4):
-                    to_slab(4 * m, red_pair.at[3], red_far.at[m - 1], rsend.at[1], rrecv.at[1])
-        count = len(chain) + len(first) + len(last)
+    def near_sums():
+        with scope("sums_near"):
+            wait_bytes(red_near, rrecv.at[0])
+            total = red_pair[2]
+            for j in range(3):
+                total = total + red_near[j]
+            red_pair[3] = total
+            for m in range(1, slabs // 4):
+                to_slab(4 * m, red_pair.at[3], red_far.at[m - 1], rsend.at[1], rrecv.at[1])
+
+    def owned(turn, plan):
+        count = sum(map(len, plan))
         with scope("rows_wait"):
             wait_bytes(rx_far.at[turn, pl.ds(0, count)], frecv.at[turn])
         total = tx_rows[turn, 0]
         for n in range(count):
             total = total + rx_far[turn, n]
-        return total
+        mine[...] = total
 
     rows_forward(0)
+    hub_sums(0, early)
 
     with scope("back_tables"):
         shape = (2 * LANES, cols)
@@ -305,7 +315,8 @@
     with jax.named_scope("weights_in"):
         lax.fori_loop(0, 8, weights_in, 0)
 
-    spectra = owned(0)
+    owned(0, early)
+    spectra = mine[...]
     for a in range(4):
         e = jnp.where(
             sub < 4,
@@ -346,21 +357,23 @@
         modes_out = modes_out + rx_chan[k]
 
     def everywhere(turn, tile):
+        rx_modes[turn, 0] = tile
+        with scope("modes_send"):
+            by_core(functools.partial(spread, turn))
+
+    def spread(turn, plan):
         rx = rx_modes.at[turn]
-        rx[0] = tile
-        with scope("modes_send"):
-            chain, first, last = main
-            order = [k for k, _ in chain[:2]] + first + [k for k, _ in chain[2:]] + last
-            kinds = [k for k, _ in chain]
-            for k in order:
-                sem = hrecv.at[turn, kinds.index(k)] if k in kinds else arecv.at[turn]
-                to_slab(k, rx.at[0], rx.at[slot_of(-k)], ssend.at[2 + turn, 0], sem)
-
-    def passed_on(turn):
+        chain, first, last = plan
+        order = [k for k, _ in chain[:2]] + first + [k for k, _ in chain[2:]] + last
+        kinds = [k for k, _ in chain]
+        for k in order:
+            sem = hrecv.at[turn, kinds.index(k)] if k in kinds else arecv.at[turn]
+            to_slab(k, rx.at[0], rx.at[slot_of(-k)], ssend.at[2 + turn, 0], sem)
+
+    def passed_on(turn, plan):
         rx = rx_modes.at[turn]
-        chain = main[0]
-        for n in list(range(2, len(chain))) + [0, 1]:
-            k, reach = chain[n]
+        by_distance = sorted(enumerate(plan[0]), key=lambda e: abs(e[1][0]))
+        for n, (k, reach) in by_distance:
             held = rx.at[slot_of(-k)]
             with scope("hub_wait"):
                 wait_bytes(held, hrecv.at[turn, n])
@@ -368,9 +381,12 @@
                 step = j if k > 0 else -j
                 to_slab(step, held, rx.at[slot_of(-k - step)], ssend.at[2 + turn, 1], arecv.at[turn])
 
+    def all_modes(turn, plan):
+        wait_bytes(rx_modes.at[turn, pl.ds(0, slabs - 1 - len(plan[0]))], arecv.at[turn])
+
     def rows_back(turn):
         with scope("modes_wait"):
-            wait_bytes(rx_modes.at[turn, pl.ds(0, slabs - 1 - len(main[0]))], arecv.at[turn])
+            by_core(functools.partial(all_modes, turn))
         with scope("back_dot"):
             found = rx_modes[turn].reshape(8 * slabs, LANES)
             both = dot3((fth[...], ftl[...]), split(found))
@@ -382,7 +398,7 @@
 
     everywhere(0, modes_out * weights)
     loads[1].wait()
-    passed_on(0)
+    by_core(functools.partial(passed_on, 0))
     rows_back(0)
 
     def gelu_chunk(a, carry):
@@ -427,7 +443,10 @@
                 device_id={"slab": me ^ j}, device_id_type=MESH,
             ).start()
 
-    g_chan[ch] = owned(1) * weights
+    by_core(functools.partial(hub_sums, 1))
+    near_sums()
+    by_core(functools.partial(owned, 1))
+    g_chan[ch] = mine[...] * weights
     for k in range(1, chans):
         to_chan(1, k, g_chan.at[ch], g_chan.at[ch]).start()
     with scope("chan_wait_two"):
@@ -481,7 +500,7 @@
 
     with scope("weights_out"):
         lax.fori_loop(0, 8, weights_out, 0)
-    passed_on(1)
+    by_core(functools.partial(passed_on, 1))
     rows_back(1)
     last_own[...] = own_g[1]
     last_rx[...] = rx_g[1]
@@ -491,14 +510,21 @@
         total = total + red_far[m]
     gate_ref[...] = total[0:1, :16]
     bgrad_ref[...] = total[1:2, :16]
-    for turn in range(2):
-        chain, first, last = main if turn else early
+    def rows_sent(turn, plan):
+        chain, first, last = plan
         wait_bytes(rx_far.at[turn, pl.ds(0, len(first) + len(last))], ssend.at[turn, 0])
         wait_bytes(tx_rows.at[turn, pl.ds(0, sum(reach for _, reach in chain))], ssend.at[turn, 1])
         wait_bytes(tx_far.at[turn, pl.ds(0, len(chain))], ssend.at[turn, 2])
-        passed = sum(reach for _, reach in main[0])
+
+    def modes_sent(turn, plan):
+        passed = sum(reach for _, reach in plan[0])
         wait_bytes(rx_modes.at[turn, pl.ds(0, slabs - 1 - passed)], ssend.at[2 + turn, 0])
         wait_bytes(rx_modes.at[turn, pl.ds(0, passed)], ssend.at[2 + turn, 1])
+
+    rows_sent(0, early)
+    by_core(functools.partial(rows_sent, 1))
+    for turn in range(2):
+        by_core(functools.partial(modes_sent, turn))
         wait_bytes(rx_chan, csend.at[turn])
     wait_bytes(red_near, rsend.at[0])
     wait_bytes(red_far, rsend.at[1])
@@ -543,7 +569,7 @@
     f32, bf16 = jnp.float32, jnp.bfloat16
     vmem, sems = pltpu.VMEM, pltpu.SemaphoreType.DMA
     hubs = slabs // 8 - 1
-    plans = early_plan(slabs), main_plan(slabs)
+    plans = early_plan(slabs), *main_plans(slabs)
     chains = max(len(p[0]) for p in plans)
     arrivals = max(sum(map(len, p)) for p in plans)
     reach = max(r for p in plans for _, r in p[0])
@@ -573,7 +599,7 @@
             vmem((2, slabs, 8, LANES), f32), vmem((2, chains, reach, 8, LANES), f32),
             vmem((2, chains, 8, LANES), f32), vmem((2, arrivals, 8, LANES), f32),
             vmem((chans, 8, LANES), f32), vmem((chans - 1, 8, LANES), f32),
-            vmem((2, slabs, 8, LANES), f32),
+            vmem((2, slabs, 8, LANES), f32), vmem((8, LANES), f32),
             vmem((2, *square), f32), vmem((2, *square), f32),
             vmem((chans, 8, LANES), f32), vmem((4, 2, LANES), f32),
             vmem((3, 2, LANES), f32), vmem((slabs // 4 - 1, 2, LANES), f32),

time: 122 us -> 120 us (0.984)
  Pallas kernels: 121 us -> 119 us
    pallas_call x1, Pallas kernels: 119 us -> 118 us  [local(): pl.pallas_call(functools.partial(kernel, (slabs, chans, modes, rows, cols...]
where the time goes in v4:
time: 120 us
  Pallas kernels  119 us (99%)
    pallas_call x1, Pallas kernels, local(): pl.pallas_call(functools.partial(kernel, (slabs, chans, modes, rows, cols...  118 us

profile of v4, /device:TPU:33, one launch (start us, length us, event | category | flops | bytes accessed | tf_op | source)
XLA Modules:
  0.0 120.0 jit_solution(8377241022510333525)
XLA Ops:
  0.6 117.8 %fno_layer.1 = (f32[512,512]{1,0:T(8,128)S(1)}, f32[512,512]{1,0:T(8,128)S(1)}, f32[16,64,64]{2,1,0:T(8,128)S(1)}, f32[1,16]{1,0:T(1,128)S(1)}, f32[1,16]{1,0:T(...) custom-call(f32[512,512]{1,0:T(8,128)} %bitcast.13, ...), custom_call_target="tpu_custom_call" | custom-call | tf_op jit(solution)/shard_map/fno_layer/pallas_call | solution.py:584
  118.5 1.6 %fno_finish.1 = (f32[512,512]{1,0:T(8,128)}, f32[512,512]{1,0:T(8,128)}, f32[16,64,64]{2,1,0:T(8,128)}, f32[1,16]{1,0:T(1,128)}, f32[1,16]{1,0:T(1,128)}) custom-call(f32[512,512]{1,0:T(8,128)S(1)} %get-tuple-element.19.ov, f32[512,512]{1,0:T(8,128)S(1)} %get-tuple-element.20.gv, f32[16,64,64]{2,1,0:T(8,128)S(1)} %get-tuple-element.21.sgv, ...), custom_call_target="tpu_custom_call" | custom-call | tf_op jit(solution)/shard_map/fno_finish/pallas_call | solution.py:619

commit v5 on v4

--- a/solution.py
+++ b/solution.py
@@ -501,9 +501,7 @@
     with scope("weights_out"):
         lax.fori_loop(0, 8, weights_out, 0)
     by_core(functools.partial(passed_on, 1))
-    rows_back(1)
-    last_own[...] = own_g[1]
-    last_rx[...] = rx_g[1]
+
     wait_bytes(red_far, rrecv.at[1])
     total = red_pair[3]
     for m in range(slabs // 4 - 1):
@@ -523,11 +521,16 @@
 
     rows_sent(0, early)
     by_core(functools.partial(rows_sent, 1))
+    by_core(functools.partial(modes_sent, 0))
     for turn in range(2):
-        by_core(functools.partial(modes_sent, turn))
         wait_bytes(rx_chan, csend.at[turn])
     wait_bytes(red_near, rsend.at[0])
     wait_bytes(red_far, rsend.at[1])
+
+    rows_back(1)
+    last_own[...] = own_g[1]
+    last_rx[...] = rx_g[1]
+    by_core(functools.partial(modes_sent, 1))
 
 
 def column_synthesis(own, theirs, a, rows, tables):

time: 120 us -> 120 us (level)
  no operation moved by 1% of the time
where the time goes in v5:
time: 120 us
  Pallas kernels  119 us (99%)
    pallas_call x1, Pallas kernels, local(): pl.pallas_call(functools.partial(kernel, (slabs, chans, modes, rows, cols...  118 us

profile of v5, /device:TPU:33, one launch (start us, length us, event | category | flops | bytes accessed | tf_op | source)
XLA Modules:
  0.0 120.0 jit_solution(8687204663905903124)
XLA Ops:
  0.6 117.8 %fno_layer.1 = (f32[512,512]{1,0:T(8,128)S(1)}, f32[512,512]{1,0:T(8,128)S(1)}, f32[16,64,64]{2,1,0:T(8,128)S(1)}, f32[1,16]{1,0:T(1,128)S(1)}, f32[1,16]{1,0:T(...) custom-call(f32[512,512]{1,0:T(8,128)} %bitcast.13, ...), custom_call_target="tpu_custom_call" | custom-call | tf_op jit(solution)/shard_map/fno_layer/pallas_call | solution.py:587
  118.4 1.6 %fno_finish.1 = (f32[512,512]{1,0:T(8,128)}, f32[512,512]{1,0:T(8,128)}, f32[16,64,64]{2,1,0:T(8,128)}, f32[1,16]{1,0:T(1,128)}, f32[1,16]{1,0:T(1,128)}) custom-call(f32[512,512]{1,0:T(8,128)S(1)} %get-tuple-element.19.ov, f32[512,512]{1,0:T(8,128)S(1)} %get-tuple-element.20.gv, f32[16,64,64]{2,1,0:T(8,128)S(1)} %get-tuple-element.21.sgv, ...), custom_call_target="tpu_custom_call" | custom-call | tf_op jit(solution)/shard_map/fno_finish/pallas_call | solution.py:622
